TPU v7x, 16 devices: a 4x2x1 block of a 4x4x8 slice. The times are simulated.
16 devices in a mesh: layer: 2 (over y, z), tensor: 8 (over x, core).
Axes of the slice: x: 4, y: 2, z: 1, core: 2. Of those that a mesh axis runs over, the one named last changes fastest.
The devices are a block of a 4x4x8 slice.
Arguments:
- gradient: bfloat16 [1024, 8192], P('layer', 'tensor'), parts along dimension 0
- left_stat: float32 [1024, 512], P(('layer', 'tensor')), parts along dimension 0
- right_stat: float32 [16384, 8192], P(('layer', 'tensor')), parts along dimension 0
- left_root: bfloat16 [1024, 512], P(('layer', 'tensor')), parts along dimension 0
- right_root: bfloat16 [16384, 8192], P(('layer', 'tensor')), parts along dimension 0
Outputs:
- output 1: float32 [1024, 512], P(('layer', 'tensor')), parts along dimension 0
- output 2: float32 [16384, 8192], P(('layer', 'tensor')), parts along dimension 0
- output 3: float32 [1024, 8192], P('layer', 'tensor'), parts along dimension 0
There are 2 independent parts. A program takes and returns all parts, laid end to end along the dimension named above; each array names one.
All inputs are finite; a program needn't handle non-finite values.
Results may differ from a plain program's by a relative error of at most 0.001.
Values are sent between devices in bfloat16 or wider.
A program may use at most 768 MiB of HBM per device.

v0:
```python
import jax
import jax.numpy as jnp
from jax import lax
from jax.sharding import PartitionSpec as P

EMA_DECAY = 0.9


def solution(mesh):
    row_spec = P(("layer", "tensor"), None)
    col_spec = P("layer", "tensor")

    def local_step(grad_local, left_block, right_block, left_root_block, right_root_block):
        grad_full = lax.all_gather(grad_local, "tensor", axis=1, tiled=True)
        left_part = jnp.einsum("mc,kc->mk", grad_local, grad_local, preferred_element_type=jnp.float32)
        left_sum = lax.psum_scatter(left_part, "tensor", scatter_dimension=0, tiled=True)
        left_new = EMA_DECAY * left_block + (1.0 - EMA_DECAY) * left_sum
        right_prod = jnp.einsum("mc,mn->cn", grad_local, grad_full, preferred_element_type=jnp.float32)
        right_new = EMA_DECAY * right_block + (1.0 - EMA_DECAY) * right_prod
        precond = jnp.einsum("mn,cn->mc", grad_full, right_root_block, preferred_element_type=jnp.float32).astype(jnp.bfloat16)
        left_root_full = lax.all_gather(left_root_block, "tensor", axis=0, tiled=True)
        direction = jnp.dot(left_root_full, precond, preferred_element_type=jnp.float32)
        return left_new, right_new, direction

    return jax.shard_map(local_step, mesh=mesh, in_specs=(col_spec, row_spec, row_spec, row_spec, row_spec), out_specs=(row_spec, row_spec, col_spec), check_vma=False)
```

profile of v0, /device:TPU:113, one launch (start us, length us, event | category | flops | bytes accessed | tf_op | source)
XLA Modules:
  0.0 143.1 jit_solution(14743327363188259000)
XLA Ops:
  7.2 0.1 reduce-scatter.2.cloned.1.call-start
  7.2 3.3 %fusion = f32[512,512]{1,0:T(8,128)} fusion(bf16[512,1024]{1,0:T(8,128)(2,1)} %param.5), kind=kOutput, calls=%fused_computation.4 | convolution fusion | flops 536870912 | bytes 2097152 | tf_op jit(solution)/shard_map/mc,kc->mk/dot_general | solution.py:15
  10.5 0.1 reduce-scatter.2.cloned.1.call-update
  10.6 0.1 all-gather.2.cloned.1.call-start
  10.6 0.7 all-gather.2.cloned.1.call-update
  11.4 19.8 %all_gather.7 = bf16[512,512]{1,0:T(8,128)(2,1)S(1)} all-gather(bf16[64,512]{1,0:T(8,128)(2,1)} %param.8), channel_id=1, replica_groups=mesh['layer'=2,'tensor'=8] {'tensor'}, dimensions={0}, use_global_device_ids=true | all-gather | bytes 589824 | tf_op jit(solution)/shard_map/all_gather | solution.py:21
  31.1 8.8 %reduce-scatter.2.cloned.1.call-done = f32[64,512]{1,0:T(8,128)} async-done(((f32[512,512]{1,0:T(8,128)}), f32[64,512]{1,0:T(8,128)}) %reduce-scatter.2.cloned.1.call-update) | async-done | bytes 131088 | tf_op jit(solution)/shard_map/reduce_scatter | solution.py:16
  39.9 1.6 %multiply_add_fusion.1 = f32[64,512]{1,0:T(8,128)} fusion(f32[64,512]{1,0:T(8,128)} %reduce-scatter.2.cloned.1.call-done, f32[64,512]{1,0:T(8,128)} %param.6), kind=kLoop, calls=%fused_computation.3 | loop fusion | flops 98304 | bytes 393216 | tf_op jit(solution)/shard_map/add | solution.py:17
  41.6 47.5 %all-gather.2.cloned.1.call-done = bf16[512,8192]{1,0:T(8,128)(2,1)} async-done(((bf16[512,1024]{1,0:T(8,128)(2,1)}), bf16[512,8192]{1,0:T(8,128)(2,1)}) %all-gather.2.cloned.1.call-update) | async-done | bytes 8388624 | tf_op jit(solution)/shard_map/all_gather | solution.py:14
  89.0 15.6 %convolution_bitcast_fusion = f32[512,1024]{0,1:T(8,128)S(1)} fusion(bf16[512,512]{1,0:T(8,128)(2,1)S(1)} %all_gather.7, bf16[512,8192]{1,0:T(8,128)(2,1)} %all-gather.2.cloned.1.call-done, bf16[1024,8192]{1,0:T(8,128)(2,1)} %param.9), kind=kOutput, calls=%fused_computation.1 | convolution fusion | flops 9127329792 | bytes 27787264 | tf_op jit(solution)/shard_map/dot_general | solution.py:22
  104.7 1.8 %copy.8 = f32[512,1024]{1,0:T(8,128)} copy(f32[512,1024]{0,1:T(8,128)S(1)} %convolution_bitcast_fusion) | data formatting | bytes 4194304
  106.5 29.8 %multiply_add_fusion = f32[1024,8192]{1,0:T(8,128)} fusion(f32[1024,8192]{1,0:T(8,128)} %param.7, bf16[512,1024]{1,0:T(8,128)(2,1)} %param.5, bf16[512,8192]{1,0:T(8,128)(2,1)} %all-gather.2.cloned.1.call-done), kind=kOutput, calls=%fused_computation | convolution fusion | flops 8615100416 | bytes 76546048 | tf_op jit(solution)/shard_map/mc,mn->cn/dot_general | solution.py:18
Async XLA Ops:
  7.2 32.7 %reduce-scatter.2.cloned.1.call-start = ((), (), s32[]{:S(2)}) async-start(), calls=%async_computation.1 | async-start | bytes 1179648 | tf_op jit(solution)/shard_map/reduce_scatter | solution.py:16
  10.6 78.5 %all-gather.2.cloned.1.call-start = ((), (), s32[]{:S(2)}) async-start(), calls=%async_computation.2 | async-start | bytes 9437184 | tf_op jit(solution)/shard_map/all_gather | solution.py:14
Sparse Core Ops, SparseCore 0:
  10.9 29.0 reduce-scatter.1
  41.5 47.4 all-gather.1
where the time goes:
time: 143 us
  waiting for transfers between devices  57 us (40%)
  matrix products  48.6 us (34%)
  blocking collectives  19.8 us (14%)
  between operations  14.1 us (10%)
  local copies, waits for them, and re-layouts  1.81 us (1%)
  other arithmetic  1.64 us (1%)
    all_gather x1, waiting for transfers between devices, local_step(): grad_full = lax.all_gather(grad_local, 'tensor', axis=1, tiled=True)  47.5 us
    dot_general x1, matrix products, local_step(): jnp.einsum('mc,mn->cn', grad_local, grad_full, preferred_element_type=jnp...  29.8 us
    all_gather x1, blocking collectives, local_step(): lax.all_gather(left_root_block, 'tensor', axis=0, tiled=True)  19.8 us
    dot_general x1, matrix products, local_step(): jnp.dot(left_root_full, precond, preferred_element_type=jnp.float32)  15.6 us
    reduce_scatter x1, waiting for transfers between devices, local_step(): lax.psum_scatter(left_part, 'tensor', scatter_dimension=0, tiled=True)  8.77 us
    dot_general x1, matrix products, local_step(): jnp.einsum('mc,kc->mk', grad_local, grad_local, preferred_element_type=jn...  3.25 us
  transfers between devices with their start and end apart: 2, of which 2 were waited for; matrix products, arithmetic and copies ran while one was open for 1% of the time, Pallas kernels for 0%

commit v1 on v0

v1 whole, which is shorter than its diff:
```python
import functools

import jax
import jax.numpy as jnp
from jax import lax
from jax.experimental import pallas as pl
from jax.experimental.pallas import tpu as pltpu
from jax.sharding import PartitionSpec as P

EMA_DECAY = 0.9
SPLIT = 4
AHEAD = 4

MESH = pl.DeviceIdType.MESH
ANY = pl.BlockSpec(memory_space=pl.ANY)
VMEM = pl.BlockSpec(memory_space=pltpu.VMEM)


def _nt(a, b):
    return lax.dot_general(a, b, (((1,), (1,)), ((), ())), preferred_element_type=jnp.float32)


def _gather_kernel(n, grad, lroot, right, rroot, rbuf, xacc, lbuf, gbuf, gt, rr,
                   own_sem, r_sem, rr_sem, recv, send_p, send_m, send_d,
                   l_own, l_recv, l_send):
    me = lax.axis_index("tensor")
    mate = me + 1 - 2 * (me % 2)
    rows, width = gbuf.shape[1], gbuf.shape[2]
    cols = gt.shape[0]
    nl = lroot.shape[0]
    hl = nl // 2
    steps = 6
    ring = lambda d: lax.rem(d + n, n)
    plus, minus = ring(me + 2), ring(me - 2)

    def slot(t, u, i):
        base = jnp.where(u == 0, me, mate)
        s = t - 2
        far = 2 + 2 * (s // SPLIT)
        owner = jnp.where(i == 0, base - far, base + far)
        part = (s + 2 * i) % SPLIT
        owner = jnp.where(t == 0, me, jnp.where(t == 1, mate, owner))
        part = jnp.where(t < 2, 2 * u + i, part)
        return lax.rem(owner + n, n) * SPLIT + part

    def span(sl):
        return pl.ds(pl.multiple_of(sl * width, width), width)

    def r_copy(sl):
        return pltpu.make_async_copy(right.at[:, span(sl)], rbuf.at[:, span(sl)], r_sem.at[sl])

    def rr_copy(sl, k):
        return pltpu.make_async_copy(rroot.at[:, span(sl)], rr.at[k, pl.ds(0, cols)], rr_sem.at[k])

    def own_copy(q):
        return pltpu.make_async_copy(grad.at[:, pl.ds(q * width, width)], gbuf.at[me * SPLIT + q], own_sem.at[q])

    def piece(sl, sem, dev):
        return pltpu.make_async_remote_copy(
            src_ref=gbuf.at[sl], dst_ref=gbuf.at[sl], send_sem=sem, recv_sem=recv.at[sl],
            device_id={"tensor": dev}, device_id_type=MESH)

    def lpart(owner, first, count, s_idx, r_idx, dev):
        at = pl.ds(pl.multiple_of(owner * nl + first, hl), count)
        return pltpu.make_async_remote_copy(
            src_ref=lbuf.at[at], dst_ref=lbuf.at[at], send_sem=l_send.at[s_idx], recv_sem=l_recv.at[r_idx],
            device_id={"tensor": dev}, device_id_type=MESH)

    own = [own_copy(q) for q in range(SPLIT)]
    for c in own:
        c.start()
    lown = pltpu.make_async_copy(lroot, lbuf.at[pl.ds(pl.multiple_of(me * nl, nl), nl)], l_own)
    lown.start()

    def loads(t, k0):
        for u in range(2):
            for i in range(2):
                sl = slot(t, u, i)
                r_copy(sl).start()
                rr_copy(sl, k0 + 2 * u + i).start()

    barrier = pltpu.get_barrier_semaphore()
    for dev in (plus, minus, mate):
        pl.semaphore_signal(barrier, inc=1, device_id={"tensor": dev}, device_id_type=MESH)
    pl.semaphore_wait(barrier, 3)

    for c in own:
        c.wait()
    lown.wait()
    sent = []
    for s in range(SPLIT):
        sent.append(piece(me * SPLIT + s, send_p.at[s], plus))
        sent.append(piece(me * SPLIT + (s + 2) % SPLIT, send_m.at[s], minus))
        sent.append(piece(me * SPLIT + s, send_d.at[s], mate))
        if s == 0:
            sent.append(lpart(me, 0, nl, 0, 0, plus))
            sent.append(lpart(me, 0, nl, 1, 1, minus))
            sent.append(lpart(me, 0, nl, 2, 4, mate))
    for c in sent:
        c.start()
    for t in range(AHEAD):
        loads(t, 4 * t)
    for q in range(SPLIT):
        gt[pl.ds(q * width, width), :] = gbuf[me * SPLIT + q].T
    xacc[...] = jnp.zeros_like(xacc)

    def unit(t, u, k0):
        sls = [slot(t, u, i) for i in range(2)]
        for sl in sls:
            r_copy(sl).wait()
            rbuf[:, span(sl)] = EMA_DECAY * rbuf[:, span(sl)] + (1.0 - EMA_DECAY) * jnp.dot(
                gt[...], gbuf[sl], preferred_element_type=jnp.float32)
        lrow = pl.ds(pl.multiple_of(me * nl, nl), nl)
        for i, sl in enumerate(sls):
            rr_copy(sl, k0 + i).wait()
            rr[k0 + i, pl.ds(cols, nl), :] = gbuf[sl, lrow, :]
        xacc[...] += _nt(rr[k0], gbuf[sls[0]]) + _nt(rr[k0 + 1], gbuf[sls[1]])

    def arrived(sl):
        piece(sl, send_d.at[0], mate).wait_recv()

    def step(t, carry):
        k0 = 4 * lax.rem(t, AHEAD)
        s = t - 2

        @pl.when(t == 1)
        def _():
            for q in range(SPLIT):
                arrived(mate * SPLIT + q)

        @pl.when(t >= 2)
        def _():
            a, b = slot(t, 0, 0), slot(t, 0, 1)
            arrived(a)
            arrived(b)

            @pl.when(s < 2)
            def _():
                piece(a, send_p.at[SPLIT + s], plus).start()
                piece(b, send_m.at[SPLIT + s], minus).start()
            piece(a, send_d.at[SPLIT + 2 * s], mate).start()
            piece(b, send_d.at[SPLIT + 2 * s + 1], mate).start()

            @pl.when(s == 1)
            def _():
                lpart(minus, 0, nl, 0, 0, plus).wait_recv()
                lpart(plus, 0, nl, 1, 1, minus).wait_recv()
                lpart(minus, 0, hl, 3, 2, plus).start()
                lpart(plus, hl, hl, 4, 3, minus).start()
                lpart(minus, 0, nl, 5, 5, mate).start()
                lpart(plus, 0, nl, 6, 6, mate).start()

            @pl.when(s == steps - 1)
            def _():
                far = ring(me + 4)
                lpart(far, 0, hl, 3, 2, plus).wait_recv()
                lpart(far, hl, hl, 4, 3, minus).wait_recv()
                lpart(far, 0, nl, 7, 7, mate).start()

        unit(t, 0, k0)

        @pl.when(t >= 2)
        def _():
            arrived(slot(t, 1, 0))
            arrived(slot(t, 1, 1))
        unit(t, 1, k0 + 2)

        @pl.when(t + AHEAD < steps + 2)
        def _():
            loads(t + AHEAD, k0)
        return carry

    lax.fori_loop(0, steps + 2, step, 0)

    for r_idx in (4, 5, 6, 7):
        lpart(me, 0, nl, 2, r_idx, mate).wait_recv()
    for s in range(steps):
        piece(me * SPLIT, send_p.at[s], plus).wait_send()
        piece(me * SPLIT, send_m.at[s], minus).wait_send()
    for s in range(SPLIT + 2 * steps):
        piece(me * SPLIT, send_d.at[s], mate).wait_send()
    for k in range(8):
        lpart(me, 0, hl if k in (3, 4) else nl, k, 0, mate).wait_send()


def _finish_kernel(xacc, lbuf, left, l_out, d_out):
    cols = d_out.shape[1]
    l_out[...] = EMA_DECAY * left[...] + (1.0 - EMA_DECAY) * xacc[pl.ds(cols, left.shape[0]), :]
    d_out[...] = _nt(lbuf[...], xacc[pl.ds(0, cols), :].astype(jnp.bfloat16))


def solution(mesh):
    row_spec = P(("layer", "tensor"), None)
    col_spec = P("layer", "tensor")
    n = mesh.shape["tensor"]

    def local_step(grad, left, right, lroot, rroot):
        rows, cols = grad.shape
        nl = lroot.shape[0]
        width = cols // SPLIT
        f32, bf16 = jnp.float32, jnp.bfloat16
        dma = pltpu.SemaphoreType.DMA
        rbuf, xacc, lbuf = pl.pallas_call(
            functools.partial(_gather_kernel, n),
            out_shape=(pltpu.VMEM(right.shape, f32), pltpu.VMEM((cols + nl, rows), f32), pltpu.VMEM((rows, rows), bf16)),
            in_specs=[ANY] * 4,
            out_specs=(VMEM,) * 3,
            scratch_shapes=[
                pltpu.VMEM((n * SPLIT, rows, width), bf16),
                pltpu.VMEM((cols, rows), bf16),
                pltpu.VMEM((4 * AHEAD, cols + nl, width), bf16),
                dma((SPLIT,)), dma((n * SPLIT,)), dma((4 * AHEAD,)), dma((n * SPLIT,)),
                dma((6,)), dma((6,)), dma((16,)),
                dma(()), dma((8,)), dma((8,)),
            ],
            compiler_params=pltpu.CompilerParams(collective_id=0, has_side_effects=True, vmem_limit_bytes=24 << 20),
        )(grad, lroot, right, rroot)
        l, d = pl.pallas_call(
            _finish_kernel,
            out_shape=(jax.ShapeDtypeStruct((nl, rows), f32), jax.ShapeDtypeStruct((rows, cols), f32)),
            in_specs=[VMEM] * 3,
            out_specs=(VMEM,) * 2,
            compiler_params=pltpu.CompilerParams(vmem_limit_bytes=8 << 20),
        )(xacc, lbuf, left)
        return l, rbuf, d

    return jax.shard_map(local_step, mesh=mesh, in_specs=(col_spec, row_spec, row_spec, row_spec, row_spec), out_specs=(row_spec, row_spec, col_spec), check_vma=False)
```

time: 143 us -> 61.8 us (0.43)
  waiting for transfers between devices: 57 us -> 0 us
  Pallas kernels: 0 us -> 48.9 us
  matrix products: 48.6 us -> 0 us
  blocking collectives: 19.8 us -> 0 us
  between operations: 14.1 us -> 0.66 us
  local copies, waits for them, and re-layouts: 1.81 us -> 11.7 us
  other arithmetic: 1.64 us -> 0 us
    pallas_call x0 -> x2, Pallas kernels: none -> 48.9 us  [the longest x1 46.9 us: local_step(): pl.pallas_call(functools.partial(_gather_kernel, n), out_shape=(pltpu.VME...]
    dot_general x3 -> x0, matrix products: 48.6 us -> none  [the longest x1 29.8 us: local_step(): jnp.einsum('mc,mn->cn', grad_local, grad_full, preferred_element_type=jnp...]
    all_gather x1 -> x0, waiting for transfers between devices: 47.5 us -> none  [local_step(): grad_full = lax.all_gather(grad_local, 'tensor', axis=1, tiled=True)]
    all_gather x1 -> x0, blocking collectives: 19.8 us -> none  [local_step(): lax.all_gather(left_root_block, 'tensor', axis=0, tiled=True)]
    unnamed x1 -> x3, local copies, waits for them, and re-layouts: 1.81 us -> 11.7 us
    reduce_scatter x1 -> x0, waiting for transfers between devices: 8.77 us -> none  [local_step(): lax.psum_scatter(left_part, 'tensor', scatter_dimension=0, tiled=True)]
    add x1 -> x0, other arithmetic: 1.64 us -> none  [local_step(): left_new = EMA_DECAY * left_block + (1.0 - EMA_DECAY) * left_sum]
  transfers between devices with their start and end apart: 2 -> 0, of which waited for: 2 -> 0; matrix products, arithmetic and copies ran while one was open for 1% -> 0% of each run, Pallas kernels for 0% -> 0%
where the time goes in v1:
time: 61.8 us; the launch traced here: 61.3 us
  Pallas kernels  48.9 us (79%)
  local copies, waits for them, and re-layouts  11.7 us (19%)
  between operations  0.66 us (1%)
    pallas_call x1, Pallas kernels, local_step(): pl.pallas_call(functools.partial(_gather_kernel, n), out_shape=(pltpu.VME...  46.9 us
    unnamed x3, local copies, waits for them, and re-layouts  11.7 us
    pallas_call x1, Pallas kernels, local_step(): pl.pallas_call(_finish_kernel, out_shape=(jax.ShapeDtypeStruct((nl, rows)...  2.07 us

profile of v1, /device:TPU:113, one launch (start us, length us, event | category | flops | bytes accessed | tf_op | source)
XLA Modules:
  0.0 61.3 jit_solution(4902990938210868716)
XLA Ops:
  0.6 0.0 copy-start
  0.6 46.9 %shard_map.76 = (f32[1024,8192]{1,0:T(8,128)S(1)}, f32[1088,512]{1,0:T(8,128)S(1)}, bf16[512,512]{1,0:T(8,128)(2,1)S(1)}) custom-call(bf16[512,1024]{1,0:T(8,128)(2,1)} %grad.1, bf16[64,512]{1,0:T(8,128)(2,1)} %lroot.1, f32[1024,8192]{1,0:T(8,128)} %right.1, bf16[1024,8192]{1,0:T(8,128)(2,1)} %rroot.1), custom_call_target="tpu_custom_call" | custom-call | tf_op jit(solution)/shard_map/pallas_call | solution.py:203
  47.5 0.0 copy-done
  47.5 2.1 %shard_map.77 = (f32[64,512]{1,0:T(8,128)}, f32[512,1024]{1,0:T(8,128)}) custom-call(f32[1088,512]{1,0:T(8,128)S(1)} %get-tuple-element.8.xacc, bf16[512,512]{1,0:T(8,128)(2,1)S(1)} %get-tuple-element.9.lbuf, f32[64,512]{1,0:T(8,128)S(1)} %copy-done), custom_call_target="tpu_custom_call" | custom-call | tf_op jit(solution)/shard_map/pallas_call | solution.py:218
  49.6 11.7 %copy.9 = f32[1024,8192]{1,0:T(8,128)} copy(f32[1024,8192]{1,0:T(8,128)S(1)} %get-tuple-element.14) | data formatting | bytes 67108864
Async XLA Ops:
  0.6 46.9 %copy-start = (f32[64,512]{1,0:T(8,128)S(1)}, f32[64,512]{1,0:T(8,128)}, u32[]{:S(2)}) copy-start(f32[64,512]{1,0:T(8,128)} %left.1) | copy-start | bytes 393220

commit v2 on v1

--- a/solution.py
+++ b/solution.py
@@ -9,7 +9,8 @@
 
 EMA_DECAY = 0.9
 SPLIT = 4
-AHEAD = 4
+AHEAD = 3
+GRANT = 12 << 20
 
 MESH = pl.DeviceIdType.MESH
 ANY = pl.BlockSpec(memory_space=pl.ANY)
@@ -18,6 +19,18 @@
 
 def _nt(a, b):
     return lax.dot_general(a, b, (((1,), (1,)), ((), ())), preferred_element_type=jnp.float32)
+
+
+def _slot(n, me, t, u, i):
+    mate = me + 1 - 2 * (me % 2)
+    base = jnp.where(u == 0, me, mate)
+    s = t - 2
+    far = 2 + 2 * (s // SPLIT)
+    owner = jnp.where(i == 0, base - far, base + far)
+    part = (s + 2 * i) % SPLIT
+    owner = jnp.where(t == 0, me, jnp.where(t == 1, mate, owner))
+    part = jnp.where(t < 2, 2 * u + i, part)
+    return lax.rem(owner + n, n) * SPLIT + part
 
 
 def _gather_kernel(n, grad, lroot, right, rroot, rbuf, xacc, lbuf, gbuf, gt, rr,
@@ -33,15 +46,7 @@
     ring = lambda d: lax.rem(d + n, n)
     plus, minus = ring(me + 2), ring(me - 2)
 
-    def slot(t, u, i):
-        base = jnp.where(u == 0, me, mate)
-        s = t - 2
-        far = 2 + 2 * (s // SPLIT)
-        owner = jnp.where(i == 0, base - far, base + far)
-        part = (s + 2 * i) % SPLIT
-        owner = jnp.where(t == 0, me, jnp.where(t == 1, mate, owner))
-        part = jnp.where(t < 2, 2 * u + i, part)
-        return lax.rem(owner + n, n) * SPLIT + part
+    slot = functools.partial(_slot, n, me)
 
     def span(sl):
         return pl.ds(pl.multiple_of(sl * width, width), width)
@@ -104,23 +109,27 @@
         gt[pl.ds(q * width, width), :] = gbuf[me * SPLIT + q].T
     xacc[...] = jnp.zeros_like(xacc)
 
+    lrow = pl.ds(pl.multiple_of(me * nl, nl), nl)
+
+    def ready(t, u, k0):
+        for i in range(2):
+            sl = slot(t, u, i)
+            r_copy(sl).wait()
+            rr_copy(sl, k0 + i).wait()
+            rr[k0 + i, pl.ds(cols, nl), :] = gbuf[sl, lrow, :]
+
     def unit(t, u, k0):
+        ready(t, u, k0)
         sls = [slot(t, u, i) for i in range(2)]
         for sl in sls:
-            r_copy(sl).wait()
             rbuf[:, span(sl)] = EMA_DECAY * rbuf[:, span(sl)] + (1.0 - EMA_DECAY) * jnp.dot(
                 gt[...], gbuf[sl], preferred_element_type=jnp.float32)
-        lrow = pl.ds(pl.multiple_of(me * nl, nl), nl)
-        for i, sl in enumerate(sls):
-            rr_copy(sl, k0 + i).wait()
-            rr[k0 + i, pl.ds(cols, nl), :] = gbuf[sl, lrow, :]
         xacc[...] += _nt(rr[k0], gbuf[sls[0]]) + _nt(rr[k0 + 1], gbuf[sls[1]])
 
     def arrived(sl):
         piece(sl, send_d.at[0], mate).wait_recv()
 
-    def step(t, carry):
-        k0 = 4 * lax.rem(t, AHEAD)
+    def take(t):
         s = t - 2
 
         @pl.when(t == 1)
@@ -157,12 +166,17 @@
                 lpart(far, hl, hl, 4, 3, minus).wait_recv()
                 lpart(far, 0, nl, 7, 7, mate).start()
 
-        unit(t, 0, k0)
-
+    def take_mate(t):
         @pl.when(t >= 2)
         def _():
             arrived(slot(t, 1, 0))
             arrived(slot(t, 1, 1))
+
+    def step(t, carry):
+        k0 = 4 * lax.rem(t, AHEAD)
+        take(t)
+        unit(t, 0, k0)
+        take_mate(t)
         unit(t, 1, k0 + 2)
 
         @pl.when(t + AHEAD < steps + 2)
@@ -170,7 +184,13 @@
             loads(t + AHEAD, k0)
         return carry
 
-    lax.fori_loop(0, steps + 2, step, 0)
+    lax.fori_loop(0, steps + 1, step, 0)
+    last = steps + 1
+    k0 = 4 * (last % AHEAD)
+    take(last)
+    ready(last, 0, k0)
+    take_mate(last)
+    ready(last, 1, k0 + 2)
 
     for r_idx in (4, 5, 6, 7):
         lpart(me, 0, nl, 2, r_idx, mate).wait_recv()
@@ -183,10 +203,41 @@
         lpart(me, 0, hl if k in (3, 4) else nl, k, 0, mate).wait_send()
 
 
-def _finish_kernel(xacc, lbuf, left, l_out, d_out):
-    cols = d_out.shape[1]
-    l_out[...] = EMA_DECAY * left[...] + (1.0 - EMA_DECAY) * xacc[pl.ds(cols, left.shape[0]), :]
-    d_out[...] = _nt(lbuf[...], xacc[pl.ds(0, cols), :].astype(jnp.bfloat16))
+def _write_kernel(n, rbuf, xacc, lbuf, gbuf, gt, rr, left, r_out, l_out, d_out,
+                  tail, xs, d_buf, l_buf, r_sem, sem):
+    me = lax.axis_index("tensor")
+    mate = me + 1 - 2 * (me % 2)
+    width = gbuf.shape[2]
+    cols, nl = d_buf.shape[1], left.shape[0]
+    last = 7
+    k0 = 4 * (last % AHEAD)
+
+    def span(sl):
+        return pl.ds(pl.multiple_of(sl * width, width), width)
+
+    tails = [_slot(n, me, last, u, i) for u in range(2) for i in range(2)]
+    copies = []
+    for t in range(last):
+        for u in range(2):
+            for i in range(2):
+                at = span(_slot(n, me, t, u, i))
+                copies.append(pltpu.make_async_copy(rbuf.at[:, at], r_out.at[:, at], r_sem.at[len(copies)]))
+                copies[-1].start()
+    for k, sl in enumerate(tails):
+        tail[k] = EMA_DECAY * rbuf[:, span(sl)] + (1.0 - EMA_DECAY) * jnp.dot(
+            gt[...], gbuf[sl], preferred_element_type=jnp.float32)
+        copies.append(pltpu.make_async_copy(tail.at[k], r_out.at[:, span(sl)], r_sem.at[len(copies)]))
+        copies[-1].start()
+    xs[...] = xacc[...] + _nt(rr[k0], gbuf[tails[0]]) + _nt(rr[k0 + 1], gbuf[tails[1]])
+    xs[...] += _nt(rr[k0 + 2], gbuf[tails[2]]) + _nt(rr[k0 + 3], gbuf[tails[3]])
+    l_buf[...] = EMA_DECAY * left[...] + (1.0 - EMA_DECAY) * xs[pl.ds(cols, nl), :]
+    d_buf[...] = _nt(lbuf[...], xs[pl.ds(0, cols), :].astype(jnp.bfloat16))
+    copies.append(pltpu.make_async_copy(l_buf, l_out, sem.at[0]))
+    copies[-1].start()
+    copies.append(pltpu.make_async_copy(d_buf, d_out, sem.at[1]))
+    copies[-1].start()
+    for c in copies:
+        c.wait()
 
 
 def solution(mesh):
@@ -200,28 +251,30 @@
         width = cols // SPLIT
         f32, bf16 = jnp.float32, jnp.bfloat16
         dma = pltpu.SemaphoreType.DMA
-        rbuf, xacc, lbuf = pl.pallas_call(
+        held = pl.pallas_call(
             functools.partial(_gather_kernel, n),
-            out_shape=(pltpu.VMEM(right.shape, f32), pltpu.VMEM((cols + nl, rows), f32), pltpu.VMEM((rows, rows), bf16)),
+            out_shape=(pltpu.VMEM(right.shape, f32), pltpu.VMEM((cols + nl, rows), f32), pltpu.VMEM((rows, rows), bf16),
+                       pltpu.VMEM((n * SPLIT, rows, width), bf16), pltpu.VMEM((cols, rows), bf16),
+                       pltpu.VMEM((4 * AHEAD, cols + nl, width), bf16)),
             in_specs=[ANY] * 4,
-            out_specs=(VMEM,) * 3,
+            out_specs=(VMEM,) * 6,
             scratch_shapes=[
-                pltpu.VMEM((n * SPLIT, rows, width), bf16),
-                pltpu.VMEM((cols, rows), bf16),
-                pltpu.VMEM((4 * AHEAD, cols + nl, width), bf16),
                 dma((SPLIT,)), dma((n * SPLIT,)), dma((4 * AHEAD,)), dma((n * SPLIT,)),
                 dma((6,)), dma((6,)), dma((16,)),
                 dma(()), dma((8,)), dma((8,)),
             ],
-            compiler_params=pltpu.CompilerParams(collective_id=0, has_side_effects=True, vmem_limit_bytes=24 << 20),
+            compiler_params=pltpu.CompilerParams(collective_id=0, has_side_effects=True, vmem_limit_bytes=GRANT),
         )(grad, lroot, right, rroot)
-        l, d = pl.pallas_call(
-            _finish_kernel,
-            out_shape=(jax.ShapeDtypeStruct((nl, rows), f32), jax.ShapeDtypeStruct((rows, cols), f32)),
-            in_specs=[VMEM] * 3,
-            out_specs=(VMEM,) * 2,
-            compiler_params=pltpu.CompilerParams(vmem_limit_bytes=8 << 20),
-        )(xacc, lbuf, left)
-        return l, rbuf, d
+        r, l, d = pl.pallas_call(
+            functools.partial(_write_kernel, n),
+            out_shape=(jax.ShapeDtypeStruct(right.shape, f32), jax.ShapeDtypeStruct((nl, rows), f32),
+                       jax.ShapeDtypeStruct((rows, cols), f32)),
+            in_specs=[VMEM] * 7,
+            out_specs=(ANY,) * 3,
+            scratch_shapes=[pltpu.VMEM((4, cols, width), f32), pltpu.VMEM((cols + nl, rows), f32),
+                            pltpu.VMEM((rows, cols), f32), pltpu.VMEM((nl, rows), f32), dma((n * SPLIT,)), dma((2,))],
+            compiler_params=pltpu.CompilerParams(vmem_limit_bytes=GRANT),
+        )(*[pltpu.with_memory_space_constraint(v, pltpu.VMEM) for v in held], left)
+        return l, r, d
 
     return jax.shard_map(local_step, mesh=mesh, in_specs=(col_spec, row_spec, row_spec, row_spec, row_spec), out_specs=(row_spec, row_spec, col_spec), check_vma=False)

time: 61.8 us -> 58.5 us (0.947)
  local copies, waits for them, and re-layouts: 11.7 us -> 0 us
  Pallas kernels: 48.9 us -> 57.7 us
    unnamed x3 -> x0, local copies, waits for them, and re-layouts: 11.7 us -> none
    pallas_call x1, Pallas kernels: 2.07 us -> 13 us  [local_step(): pl.pallas_call(functools.partial(_write_kernel, n), out_shape=(jax.ShapeD...]
    pallas_call x1, Pallas kernels: 46.9 us -> 44.7 us  [local_step(): pl.pallas_call(functools.partial(_gather_kernel, n), out_shape=(pltpu.VME...]
where the time goes in v2:
time: 58.5 us; the launch traced here: 58.3 us
  Pallas kernels  57.7 us (99%)
  between operations  0.64 us (1%)
    pallas_call x1, Pallas kernels, local_step(): pl.pallas_call(functools.partial(_gather_kernel, n), out_shape=(pltpu.VME...  44.7 us
    pallas_call x1, Pallas kernels, local_step(): pl.pallas_call(functools.partial(_write_kernel, n), out_shape=(jax.ShapeD...  13 us

profile of v2, /device:TPU:113, one launch (start us, length us, event | category | flops | bytes accessed | tf_op | source)
XLA Modules:
  0.0 58.3 jit_solution(7314946455592372441)
XLA Ops:
  0.6 44.7 %shard_map.76 = (f32[1024,8192]{1,0:T(8,128)S(1)}, f32[1088,512]{1,0:T(8,128)S(1)}, bf16[512,512]{1,0:T(8,128)(2,1)S(1)}, bf16[32,512,256]{2,1,0:T(8,128)(2,1)S(...) custom-call(bf16[512,1024]{1,0:T(8,128)(2,1)} %grad.1, bf16[64,512]{1,0:T(8,128)(2,1)} %lroot.1, ...), custom_call_target="tpu_custom_call" | custom-call | tf_op jit(solution)/shard_map/pallas_call | solution.py:254
  45.3 13.0 %shard_map.77 = (f32[1024,8192]{1,0:T(8,128)}, f32[64,512]{1,0:T(8,128)}, f32[512,1024]{1,0:T(8,128)}) custom-call(f32[1024,8192]{1,0:T(8,128)S(1)} %get-tuple-element.12.rbuf, f32[1088,512]{1,0:T(8,128)S(1)} %get-tuple-element.13.xacc, bf16[512,512]{1,0:T(8,128)(2,1)S(1)} %get-tuple-element.14.lbuf, bf16[32,512,256]{2,1,0:T(8,128)(2,1)S(1)} %get-tuple-element.15.gbuf, ...), custom_call_target="tpu_custom_call" | custom-call | tf_op jit(solution)/shard_map/pallas_call | solution.py:268

commit v3 on v2

--- a/solution.py
+++ b/solution.py
@@ -222,20 +222,20 @@
             for i in range(2):
                 at = span(_slot(n, me, t, u, i))
                 copies.append(pltpu.make_async_copy(rbuf.at[:, at], r_out.at[:, at], r_sem.at[len(copies)]))
-                copies[-1].start()
+                copies[-1].start(priority=len(copies) % 2)
     for k, sl in enumerate(tails):
         tail[k] = EMA_DECAY * rbuf[:, span(sl)] + (1.0 - EMA_DECAY) * jnp.dot(
             gt[...], gbuf[sl], preferred_element_type=jnp.float32)
         copies.append(pltpu.make_async_copy(tail.at[k], r_out.at[:, span(sl)], r_sem.at[len(copies)]))
-        copies[-1].start()
+        copies[-1].start(priority=len(copies) % 2)
     xs[...] = xacc[...] + _nt(rr[k0], gbuf[tails[0]]) + _nt(rr[k0 + 1], gbuf[tails[1]])
     xs[...] += _nt(rr[k0 + 2], gbuf[tails[2]]) + _nt(rr[k0 + 3], gbuf[tails[3]])
     l_buf[...] = EMA_DECAY * left[...] + (1.0 - EMA_DECAY) * xs[pl.ds(cols, nl), :]
     d_buf[...] = _nt(lbuf[...], xs[pl.ds(0, cols), :].astype(jnp.bfloat16))
     copies.append(pltpu.make_async_copy(l_buf, l_out, sem.at[0]))
-    copies[-1].start()
+    copies[-1].start(priority=len(copies) % 2)
     copies.append(pltpu.make_async_copy(d_buf, d_out, sem.at[1]))
-    copies[-1].start()
+    copies[-1].start(priority=len(copies) % 2)
     for c in copies:
         c.wait()
 

time: 58.5 us -> 58.4 us (level)
  no operation moved by 1% of the time
where the time goes in v3:
time: 58.4 us; the launch traced here: 58.3 us
  Pallas kernels  57.6 us (99%)
  between operations  0.64 us (1%)
    pallas_call x1, Pallas kernels, local_step(): pl.pallas_call(functools.partial(_gather_kernel, n), out_shape=(pltpu.VME...  44.7 us
    pallas_call x1, Pallas kernels, local_step(): pl.pallas_call(functools.partial(_write_kernel, n), out_shape=(jax.ShapeD...  12.9 us

profile of v3, /device:TPU:113, one launch (start us, length us, event | category | flops | bytes accessed | tf_op | source)
XLA Modules:
  0.0 58.3 jit_solution(13153399525639966136)
XLA Ops:
  0.6 44.7 %shard_map.76 = (f32[1024,8192]{1,0:T(8,128)S(1)}, f32[1088,512]{1,0:T(8,128)S(1)}, bf16[512,512]{1,0:T(8,128)(2,1)S(1)}, bf16[32,512,256]{2,1,0:T(8,128)(2,1)S(...) custom-call(bf16[512,1024]{1,0:T(8,128)(2,1)} %grad.1, bf16[64,512]{1,0:T(8,128)(2,1)} %lroot.1, ...), custom_call_target="tpu_custom_call" | custom-call | tf_op jit(solution)/shard_map/pallas_call | solution.py:254
  45.3 12.9 %shard_map.77 = (f32[1024,8192]{1,0:T(8,128)}, f32[64,512]{1,0:T(8,128)}, f32[512,1024]{1,0:T(8,128)}) custom-call(f32[1024,8192]{1,0:T(8,128)S(1)} %get-tuple-element.12.rbuf, f32[1088,512]{1,0:T(8,128)S(1)} %get-tuple-element.13.xacc, bf16[512,512]{1,0:T(8,128)(2,1)S(1)} %get-tuple-element.14.lbuf, bf16[32,512,256]{2,1,0:T(8,128)(2,1)S(1)} %get-tuple-element.15.gbuf, ...), custom_call_target="tpu_custom_call" | custom-call | tf_op jit(solution)/shard_map/pallas_call | solution.py:268

commit v4 on v0

v4 whole, which is shorter than its diff:
```python
import jax
import jax.numpy as jnp
from jax import lax
from jax.experimental import pallas as pl
from jax.experimental.pallas import tpu as pltpu
from jax.sharding import PartitionSpec as P


EMA_DECAY = 0.9
WIDTH = 256
GRANT = 14 << 20


ANY = pl.BlockSpec(memory_space=pl.ANY)
VMEM = pl.BlockSpec(memory_space=pltpu.VMEM)


def _nt(a, b):
    return lax.dot_general(a, b, (((1,), (1,)), ((), ())), preferred_element_type=jnp.float32)


def _places(n, me, where, cols, span):
    mate = me + 1 - 2 * (me % 2)
    owners = [lax.rem((mate if swapped else me) + shift, n) for swapped, shift, _ in where]
    return owners, [owner * cols + half * span for owner, (_, _, half) in zip(owners, where)]


def _unit_kernel(n, where, nxt, *refs):
    refs = list(refs)
    m = len(where)
    first, last = refs.pop(0), refs.pop(0)
    take = lambda k: [refs.pop(0) for _ in range(k)]
    if not first:
        take(1)
    right, rroot, gt = take(3)
    chunks = take(m)
    if not first:
        r_in, rr_in, x_prev, l_prev = take(4)
    if last:
        left, r_out, l_out, d_out = take(4)
    else:
        r_out, r_next, rr_next, xs, lbuf = take(5)
    stage, w_sem, r_sem, rr_sem = take(4)
    if first:
        r_in, rr_in = take(2)
    if last:
        xs, lbuf, d_buf, l_buf, sem = take(5)
    me = lax.axis_index("tensor")
    cols, rows = gt.shape
    span = chunks[0].shape[1]
    nl = rows // n
    lrow = pl.ds(pl.multiple_of(me * nl, nl), nl)
    per = span // WIDTH

    def loads(places, r_to, rr_to, base):
        out = []
        for k, c0 in enumerate(places):
            for i in range(per):
                at = pl.ds(pl.multiple_of(c0 + i * WIDTH, WIDTH), WIDTH)
                s = k * per + i
                out.append(pltpu.make_async_copy(right.at[:, at], r_to.at[s], r_sem.at[base + s]))
            at = pl.ds(pl.multiple_of(c0, span), span)
            out.append(pltpu.make_async_copy(rroot.at[:, at], rr_to.at[k, pl.ds(0, cols)], rr_sem.at[base // per + k]))
        for c in out:
            c.start()
        return out

    owners, places = _places(n, me, where, cols, span)
    if first:
        mine = loads(places, r_in, rr_in, m * per)
    ahead = [] if last else loads(_places(n, me, nxt, cols, span)[1], r_next, rr_next, 0)
    if first:
        for c in mine:
            c.wait()
    if not first:
        lbuf[...] = l_prev[...]
    writes = []
    for k in range(m):
        for i in range(per):
            at = pl.ds(pl.multiple_of(places[k] + i * WIDTH, WIDTH), WIDTH)
            s = k * per + i
            stage[s] = EMA_DECAY * r_in[s] + (1.0 - EMA_DECAY) * jnp.dot(
                gt[...], chunks[k][pl.ds(0, rows), pl.ds(i * WIDTH, WIDTH)], preferred_element_type=jnp.float32)
            writes.append(pltpu.make_async_copy(stage.at[s], r_out.at[:, at], w_sem.at[s]))
            writes[-1].start()
    for k in range(m):
        if chunks[k].shape[0] > rows:
            lbuf[pl.ds(pl.multiple_of(owners[k] * nl, nl), nl), :] = chunks[k][pl.ds(rows, nl), :]
        h = chunks[k][pl.ds(0, rows), :]
        x_term, l_term = _nt(rr_in[k, pl.ds(0, cols)], h), _nt(chunks[k][lrow, :], h)
        top, low = pl.ds(0, cols), pl.ds(cols, nl)
        if k == 0 and first:
            xs[top, :], xs[low, :] = x_term, l_term
        else:
            old = xs if k else x_prev
            xs[top, :] = old[top, :] + x_term
            xs[low, :] = old[low, :] + l_term
    if last:
        d_buf[...] = _nt(lbuf[...], xs[pl.ds(0, cols), :].astype(jnp.bfloat16))
        writes.append(pltpu.make_async_copy(d_buf, d_out, sem.at[0]))
        writes[-1].start()
        l_buf[...] = EMA_DECAY * left[...] + (1.0 - EMA_DECAY) * xs[pl.ds(cols, nl), :]
        writes.append(pltpu.make_async_copy(l_buf, l_out, sem.at[1]))
        writes[-1].start()
    for w in writes + ahead:
        w.wait()


def _on_chip(v):
    return pltpu.with_memory_space_constraint(v, pltpu.VMEM)


def _unit(n, where, nxt, state, right, rroot, gt, chunks, left=None):
    first, last = state is None, left is not None
    m = len(where)
    cols, rows = gt.shape
    span = chunks[0].shape[1]
    nl = rows // n
    f32, bf16 = jnp.float32, gt.dtype
    dma = pltpu.SemaphoreType.DMA
    slabs = m * span // WIDTH
    args, specs = ([], []) if first else ([state[0]], [ANY])
    args += [right, rroot, gt, *[_on_chip(c) for c in chunks]]
    specs += [ANY, ANY, VMEM] + [VMEM] * m
    alias = {} if first else {0: 0}
    r_shape = jax.ShapeDtypeStruct(rroot.shape, f32)
    held = ((slabs, cols, WIDTH), f32), ((m, cols, span), bf16), ((cols + nl, rows), f32), ((rows, rows), bf16)
    scratch = [pltpu.VMEM((slabs, cols, WIDTH), f32), dma((slabs,)), dma((2 * slabs,)), dma((2 * m,))]
    if first:
        scratch += [pltpu.VMEM(*held[0]), pltpu.VMEM(*held[1])]
    else:
        if not last:
            alias.update({len(args) + 2: 3, len(args) + 3: 4})
        args += [_on_chip(v) for v in state[1:]]
        specs += [VMEM] * 4
    if last:
        args.append(left)
        specs.append(VMEM)
        out_shape = (r_shape, jax.ShapeDtypeStruct((nl, rows), f32), jax.ShapeDtypeStruct((rows, cols), f32))
        out_specs = (ANY,) * 3
        scratch += [pltpu.VMEM(*held[2]), pltpu.VMEM(*held[3]), pltpu.VMEM((rows, cols), f32),
                    pltpu.VMEM((nl, rows), f32), dma((2,))]
    else:
        out_shape = (r_shape, *[pltpu.VMEM(*h) for h in held])
        out_specs = (ANY,) + (VMEM,) * 4
    flops = 4 * rows * cols * m * span
    return pl.pallas_call(
        lambda *refs: _unit_kernel(n, where, nxt, first, last, *refs),
        out_shape=out_shape, in_specs=specs, out_specs=out_specs, scratch_shapes=scratch, input_output_aliases=alias,
        compiler_params=pltpu.CompilerParams(vmem_limit_bytes=GRANT),
        cost_estimate=pl.CostEstimate(flops=flops, bytes_accessed=m * span * cols * 10, transcendentals=0),
    )(*args)


def solution(mesh):
    row_spec = P(("layer", "tensor"), None)
    col_spec = P("layer", "tensor")
    n = mesh.shape["tensor"]

    def shift(v, k):
        return lax.ppermute(v, "tensor", [(j, (j + k) % n) for j in range(n)])

    def swap(v):
        return lax.ppermute(v, "tensor", [(j, j ^ 1) for j in range(n)])

    def after(vals, state):
        out = lax.optimization_barrier((*vals, state[3], state[4]))
        return out[:-2], (*state[:3], *out[-2:])

    def both(swapped, da, ha, db, hb):
        return [(swapped, da % n, ha), (swapped, db % n, hb)]

    def group_step(grad, left, right, lroot, rroot):
        _, cols = grad.shape
        half = cols // 2
        p0, p1 = grad[:, :half], grad[:, half:]
        u0 = jnp.concatenate([p0, lroot], axis=0)
        u1 = jnp.concatenate([p1, lroot], axis=0)
        a0, b0 = shift(u0, 2), shift(u1, n - 2)
        a1, b1 = shift(p1, 2), shift(p0, n - 2)
        s = swap(u0), swap(u1)
        gt = _on_chip(grad.T)
        right, rroot = (pltpu.with_memory_space_constraint(v, pltpu.HBM) for v in (right, rroot))
        plan = [[(False, 0, 0), (False, 0, 1)], [(True, 0, 0), (True, 0, 1)]]
        for args in ((-2, 0, 2, 1), (-2, 1, 2, 0), (-4, 0, 4, 1)):
            plan += [both(False, *args), both(True, *args)]
        plan.append(None)

        def unit(k, state, chunks, *tail):
            return _unit(n, plan[k], plan[k + 1], state, right, rroot, gt, chunks, *tail)

        st = unit(0, None, [u0, u1])
        s, st = after(s, st)
        st = unit(1, st, s)
        (a0, b0), st = after((a0, b0), st)
        f = shift(a0, 2), shift(b0, n - 2)
        for k, got in ((2, (a0, b0)), (4, (a1, b1)), (6, f)):
            if k > 2:
                got, st = after(got, st)
            s = swap(got[0]), swap(got[1])
            st = unit(k, st, got)
            s, st = after(s, st)
            st = unit(k + 1, st, s, *([left] if k == 6 else []))
        r, l, d = st
        return l, r, d

    return jax.shard_map(group_step, mesh=mesh, in_specs=(col_spec, row_spec, row_spec, row_spec, row_spec), out_specs=(row_spec, row_spec, col_spec), check_vma=False)
```

time: 143 us -> 70.2 us (0.49)
  waiting for transfers between devices: 57 us -> 0.26 us
  Pallas kernels: 0 us -> 51 us
  matrix products: 48.6 us -> 0 us
  blocking collectives: 19.8 us -> 0 us
  starting transfers between devices: 0.13 us -> 13.9 us
  between operations: 14.1 us -> 1.01 us
    pallas_call x0 -> x8, Pallas kernels: none -> 51 us  [_unit(): pl.pallas_call(lambda *refs: _unit_kernel(n, where, nxt, first, last, *re...]
    dot_general x3 -> x0, matrix products: 48.6 us -> none  [the longest x1 29.8 us: local_step(): jnp.einsum('mc,mn->cn', grad_local, grad_full, preferred_element_type=jnp...]
    all_gather x1 -> x0, waiting for transfers between devices: 47.5 us -> none  [local_step(): grad_full = lax.all_gather(grad_local, 'tensor', axis=1, tiled=True)]
    all_gather x1 -> x0, blocking collectives: 19.8 us -> none  [local_step(): lax.all_gather(left_root_block, 'tensor', axis=0, tiled=True)]
    ppermute x0 -> x14, starting transfers between devices: none -> 13.9 us  [the longest x6 8.95 us: shift(): return lax.ppermute(v, 'tensor', [(j, (j + k) % n) for j in range(n)])]
    reduce_scatter x1 -> x0, waiting for transfers between devices: 8.77 us -> none  [local_step(): lax.psum_scatter(left_part, 'tensor', scatter_dimension=0, tiled=True)]
    add x1 -> x0, other arithmetic: 1.64 us -> none  [local_step(): left_new = EMA_DECAY * left_block + (1.0 - EMA_DECAY) * left_sum]
  transfers between devices with their start and end apart: 2 -> 14, of which waited for: 2 -> 1; matrix products, arithmetic and copies ran while one was open for 1% -> 2% of each run, Pallas kernels for 0% -> 65%
where the time goes in v4:
time: 70.2 us; the launch traced here: 70 us
  Pallas kernels  51 us (73%)
  starting transfers between devices  13.9 us (20%)
  local copies, waits for them, and re-layouts  2.8 us (4%)
  other arithmetic  1.01 us (1%)
  between operations  1.01 us (1%)
    pallas_call x8, Pallas kernels, _unit(): pl.pallas_call(lambda *refs: _unit_kernel(n, where, nxt, first, last, *re...  51 us
    ppermute x6, starting transfers between devices, shift(): return lax.ppermute(v, 'tensor', [(j, (j + k) % n) for j in range(n)])  8.95 us
    ppermute x8, starting transfers between devices, swap(): return lax.ppermute(v, 'tensor', [(j, j ^ 1) for j in range(n)])  4.94 us
    unnamed x11, local copies, waits for them, and re-layouts  1.52 us
  transfers between devices with their start and end apart: 14, of which 1 were waited for; matrix products, arithmetic and copies ran while one was open for 2% of the time, Pallas kernels for 65%

profile of v4, /device:TPU:113, one launch (start us, length us, event | category | flops | bytes accessed | tf_op | source)
XLA Modules:
  0.0 70.0 jit_solution(5819605928742259076)
XLA Ops:
  0.6 1.3 %fusion = (bf16[512,512]{1,0:T(8,128)(2,1)S(1)}, bf16[512,512]{1,0:T(8,128)(2,1)S(1)}) fusion(bf16[512,1024]{1,0:T(8,128)(2,1)} %param.5), kind=kLoop, calls=%fused_computation.2 | loop fusion | bytes 2097152 | tf_op jit(solution)/shard_map/slice | solution.py:176
  1.9 0.0 copy-start.1
  1.9 0.0 copy-start.3
  1.9 1.0 %pad_maximum_fusion = (bf16[576,512]{1,0:T(8,128)(2,1)S(1)}, bf16[576,512]{1,0:T(8,128)(2,1)S(1)}) fusion(bf16[64,512]{1,0:T(8,128)(2,1)} %param.8, bf16[512,512]{1,0:T(8,128)(2,1)S(1)} %get-tuple-element.135, bf16[512,512]{1,0:T(8,128)(2,1)S(1)} %get-tuple-element.136), kind=kLoop, calls=%fused_computation | loop fusion | flops 2064384 | bytes 2293760 | tf_op jit(solution)/shard_map/concatenate | solution.py:178
  2.9 0.8 %collective-permute-start.1 = (bf16[576,512]{1,0:T(8,128)(2,1)S(1)}, bf16[576,512]{1,0:T(8,128)(2,1)}, u32[]{:S(2)}, u32[]{:S(2)}) collective-permute-start(bf16[576,512]{1,0:T(8,128)(2,1)S(1)} %get-tuple-element.137.refs_4_), channel_id=1, source_target_pairs={{0,1},{1,0},{2,3},{3,2},{4,5},{5,4},{6,7},{7,6},{8,9},{9,8},{10,11... | collective-permute-start | bytes 1769480 | tf_op jit(solution)/shard_map/ppermute | solution.py:164
  3.7 0.1 collective-permute-start
  3.8 3.6 %collective-permute-start.3 = (bf16[576,512]{1,0:T(8,128)(2,1)S(1)}, bf16[576,512]{1,0:T(8,128)(2,1)S(1)}, u32[]{:S(2)}, u32[]{:S(2)}) collective-permute-start(bf16[576,512]{1,0:T(8,128)(2,1)S(1)} %get-tuple-element.137.refs_4_), channel_id=1, source_target_pairs={{0,6},{1,7},{2,0},{3,1},{4,2},{5,3},{6,4},{7,5},{8,14},{9,15},{10,... | collective-permute-start | bytes 1769480 | tf_op jit(solution)/shard_map/ppermute | solution.py:161
  7.4 0.0 copy-done.1
  7.4 0.0 copy-done.3
  7.4 0.0 collective-permute-start.2
  7.4 1.5 %copy.27 = bf16[512,1024]{0,1:T(8,128)(2,1)S(1)} copy(bf16[512,1024]{1,0:T(8,128)(2,1)} %param.5) | data formatting | bytes 2097152 | tf_op args[0]
  8.9 6.1 %shard_map.76 = (f32[1024,8192]{1,0:T(8,128)}, f32[4,1024,256]{2,1,0:T(8,128)S(1)}, bf16[2,1024,512]{2,1,0:T(8,128)(2,1)S(1)}, f32[1088,512]{1,0:T(8,128)S(1)}, bf16[512,512]{1,0:T(8,128)(2,1)S(1)}) custom-call(f32[1024,8192]{1,0:T(8,128)} %refs_1_.15, bf16[1024,8192]{1,0:T(8,128)(2,1)} %refs_2_.13, bf16[1024,512]{1,0:T(8,128)(2,1)S(1)} %bitcast.1, ...), custom_call_target="tpu_custom_call" | custom-call | flops 2147483648 | bytes 10485760 | tf_op jit(solution)/shard_map/pallas_call | solution.py:147
  15.0 0.0 collective-permute-done.1.refs_5_
  15.0 0.0 collective-permute-done.refs_4_
  15.0 0.0 copy-start.4
  15.0 0.0 copy-start.2
  15.1 7.7 %shard_map.77 = (f32[1024,8192]{1,0:T(8,128)}, f32[4,1024,256]{2,1,0:T(8,128)S(1)}, bf16[2,1024,512]{2,1,0:T(8,128)(2,1)S(1)}, f32[1088,512]{1,0:T(8,128)S(1)}, bf16[512,512]{1,0:T(8,128)(2,1)S(1)}) custom-call(f32[1024,8192]{1,0:T(8,128)} %get-tuple-element.69.refs_0_, ...), custom_call_target="tpu_custom_call", output_to_operand_aliasing={{0}: (0, {}), {3}: (8, {}), {4}: (9, {})} | custom-call | flops 2147483648 | bytes 10485760 | tf_op jit(solution)/shard_map/pallas_call | solution.py:147
  22.8 0.0 collective-permute-done.3.refs_5_
  22.8 0.0 collective-permute-done.2.refs_4_
  22.8 1.6 %collective-permute-start.4 = (bf16[576,512]{1,0:T(8,128)(2,1)S(1)}, bf16[576,512]{1,0:T(8,128)(2,1)S(1)}, u32[]{:S(2)}, u32[]{:S(2)}) collective-permute-start(bf16[576,512]{1,0:T(8,128)(2,1)S(1)} %collective-permute-done.2.refs_4_), channel_id=1, source_target_pairs={{0,1},{1,0},{2,3},{3,2},{4,5},{5,4},{6,7},{7,6},{8,9},{9,8},{10,11... | collective-permute-start | bytes 1769480 | tf_op jit(solution)/shard_map/ppermute | solution.py:164
  24.4 0.0 collective-permute-start.5
  24.4 0.0 copy-done.4
  24.4 0.0 collective-permute-start.6
  24.4 0.0 copy-done.2
  24.4 2.7 %collective-permute-start.7 = (bf16[512,512]{1,0:T(8,128)(2,1)S(1)}, bf16[512,512]{1,0:T(8,128)(2,1)S(1)}, u32[]{:S(2)}, u32[]{:S(2)}) collective-permute-start(bf16[512,512]{1,0:T(8,128)(2,1)S(1)} %copy-done.2), channel_id=1, source_target_pairs={{0,6},{1,7},{2,0},{3,1},{4,2},{5,3},{6,4},{7,5},{8,14},{9,15},{10,... | collective-permute-start | bytes 1572872 | tf_op jit(solution)/shard_map/ppermute | solution.py:161
  27.1 6.4 %shard_map.78 = (f32[1024,8192]{1,0:T(8,128)}, f32[4,1024,256]{2,1,0:T(8,128)S(1)}, bf16[2,1024,512]{2,1,0:T(8,128)(2,1)S(1)}, f32[1088,512]{1,0:T(8,128)S(1)}, bf16[512,512]{1,0:T(8,128)(2,1)S(1)}) custom-call(f32[1024,8192]{1,0:T(8,128)} %get-tuple-element.78.refs_0_, ...), custom_call_target="tpu_custom_call", output_to_operand_aliasing={{0}: (0, {}), {3}: (8, {}), {4}: (9, {})} | custom-call | flops 2147483648 | bytes 10485760 | tf_op jit(solution)/shard_map/pallas_call | solution.py:147
  33.5 0.0 collective-permute-done.4.refs_4_
  33.5 0.0 collective-permute-done.5.refs_5_
  33.5 6.4 %shard_map.79 = (f32[1024,8192]{1,0:T(8,128)}, f32[4,1024,256]{2,1,0:T(8,128)S(1)}, bf16[2,1024,512]{2,1,0:T(8,128)(2,1)S(1)}, f32[1088,512]{1,0:T(8,128)S(1)}, bf16[512,512]{1,0:T(8,128)(2,1)S(1)}) custom-call(f32[1024,8192]{1,0:T(8,128)} %get-tuple-element.87.refs_0_, ...), custom_call_target="tpu_custom_call", output_to_operand_aliasing={{0}: (0, {}), {3}: (8, {}), {4}: (9, {})} | custom-call | flops 2147483648 | bytes 10485760 | tf_op jit(solution)/shard_map/pallas_call | solution.py:147
  39.9 0.0 collective-permute-done.6.refs_4_
  40.0 0.0 collective-permute-done.7.refs_5_
  40.0 1.1 %collective-permute-start.8 = (bf16[512,512]{1,0:T(8,128)(2,1)S(1)}, bf16[512,512]{1,0:T(8,128)(2,1)S(1)}, u32[]{:S(2)}, u32[]{:S(2)}) collective-permute-start(bf16[512,512]{1,0:T(8,128)(2,1)S(1)} %collective-permute-done.6.refs_4_), channel_id=1, source_target_pairs={{0,1},{1,0},{2,3},{3,2},{4,5},{5,4},{6,7},{7,6},{8,9},{9,8},{10,11... | collective-permute-start | bytes 1572872 | tf_op jit(solution)/shard_map/ppermute | solution.py:164
  41.1 0.1 collective-permute-start.9
  41.2 0.0 collective-permute-start.10
  41.2 2.7 %collective-permute-start.11 = (bf16[576,512]{1,0:T(8,128)(2,1)S(1)}, bf16[576,512]{1,0:T(8,128)(2,1)S(1)}, u32[]{:S(2)}, u32[]{:S(2)}) collective-permute-start(bf16[576,512]{1,0:T(8,128)(2,1)S(1)} %collective-permute-done.3.refs_5_), channel_id=1, source_target_pairs={{0,6},{1,7},{2,0},{3,1},{4,2},{5,3},{6,4},{7,5},{8,14},{9,15},{10,... | collective-permute-start | bytes 1769480 | tf_op jit(solution)/shard_map/ppermute | solution.py:161
  43.9 6.3 %shard_map.80 = (f32[1024,8192]{1,0:T(8,128)}, f32[4,1024,256]{2,1,0:T(8,128)S(1)}, bf16[2,1024,512]{2,1,0:T(8,128)(2,1)S(1)}, f32[1088,512]{1,0:T(8,128)S(1)}, bf16[512,512]{1,0:T(8,128)(2,1)S(1)}) custom-call(f32[1024,8192]{1,0:T(8,128)} %get-tuple-element.96.refs_0_, ...), custom_call_target="tpu_custom_call", output_to_operand_aliasing={{0}: (0, {}), {3}: (8, {}), {4}: (9, {})} | custom-call | flops 2147483648 | bytes 10485760 | tf_op jit(solution)/shard_map/pallas_call | solution.py:147
  50.2 0.0 collective-permute-done.8.refs_4_
  50.2 0.0 collective-permute-done.9.refs_5_
  50.2 6.5 %shard_map.81 = (f32[1024,8192]{1,0:T(8,128)}, f32[4,1024,256]{2,1,0:T(8,128)S(1)}, bf16[2,1024,512]{2,1,0:T(8,128)(2,1)S(1)}, f32[1088,512]{1,0:T(8,128)S(1)}, bf16[512,512]{1,0:T(8,128)(2,1)S(1)}) custom-call(f32[1024,8192]{1,0:T(8,128)} %get-tuple-element.105.refs_0_, ...), custom_call_target="tpu_custom_call", output_to_operand_aliasing={{0}: (0, {}), {3}: (8, {}), {4}: (9, {})} | custom-call | flops 2147483648 | bytes 10485760 | tf_op jit(solution)/shard_map/pallas_call | solution.py:147
  56.7 0.2 collective-permute-done.10.refs_4_
  56.9 0.0 collective-permute-done.11.refs_5_
  56.9 1.3 %collective-permute-start.12 = (bf16[576,512]{1,0:T(8,128)(2,1)S(1)}, bf16[576,512]{1,0:T(8,128)(2,1)S(1)}, u32[]{:S(2)}, u32[]{:S(2)}) collective-permute-start(bf16[576,512]{1,0:T(8,128)(2,1)S(1)} %collective-permute-done.10.refs_4_), channel_id=1, source_target_pairs={{0,1},{1,0},{2,3},{3,2},{4,5},{5,4},{6,7},{7,6},{8,9},{9,8},{10,11... | collective-permute-start | bytes 1769480 | tf_op jit(solution)/shard_map/ppermute | solution.py:164
  58.2 0.0 collective-permute-start.13
  58.2 0.0 copy-start
  58.2 6.4 %shard_map.82 = (f32[1024,8192]{1,0:T(8,128)}, f32[4,1024,256]{2,1,0:T(8,128)S(1)}, bf16[2,1024,512]{2,1,0:T(8,128)(2,1)S(1)}, f32[1088,512]{1,0:T(8,128)S(1)}, bf16[512,512]{1,0:T(8,128)(2,1)S(1)}) custom-call(f32[1024,8192]{1,0:T(8,128)} %get-tuple-element.114.refs_0_, ...), custom_call_target="tpu_custom_call", output_to_operand_aliasing={{0}: (0, {}), {3}: (8, {}), {4}: (9, {})} | custom-call | flops 2147483648 | bytes 10485760 | tf_op jit(solution)/shard_map/pallas_call | solution.py:147
  64.6 0.0 collective-permute-done.12.refs_4_
  64.6 0.0 collective-permute-done.13.refs_5_
  64.6 0.0 copy-done
  64.6 5.2 %shard_map.83 = (f32[1024,8192]{1,0:T(8,128)}, f32[64,512]{1,0:T(8,128)}, f32[512,1024]{1,0:T(8,128)}) custom-call(f32[1024,8192]{1,0:T(8,128)} %get-tuple-element.123.refs_0_, f32[1024,8192]{1,0:T(8,128)} %refs_1_.15, bf16[1024,8192]{1,0:T(8,128)(2,1)} %refs_2_.13, bf16[1024,512]{1,0:T(8,128)(2,1)S(1)} %bitcast.8, ...), custom_call_target="tpu_custom_call", output_to_operand_aliasing={{0}: (0, {})} | custom-call | flops 2147483648 | bytes 10485760 | tf_op jit(solution)/shard_map/pallas_call | solution.py:147
Async XLA Ops:
  1.9 5.5 %copy-start.1 = (bf16[512,512]{1,0:T(8,128)(2,1)}, bf16[512,512]{1,0:T(8,128)(2,1)S(1)}, u32[]{:S(2)}) copy-start(bf16[512,512]{1,0:T(8,128)(2,1)S(1)} %get-tuple-element.136) | copy-start | bytes 1572868
  1.9 5.5 %copy-start.3 = (bf16[512,512]{1,0:T(8,128)(2,1)}, bf16[512,512]{1,0:T(8,128)(2,1)S(1)}, u32[]{:S(2)}) copy-start(bf16[512,512]{1,0:T(8,128)(2,1)S(1)} %get-tuple-element.135) | copy-start | bytes 1572868
  2.9 12.1 %collective-permute-start.1 = (bf16[576,512]{1,0:T(8,128)(2,1)S(1)}, bf16[576,512]{1,0:T(8,128)(2,1)}, u32[]{:S(2)}, u32[]{:S(2)}) collective-permute-start(bf16[576,512]{1,0:T(8,128)(2,1)S(1)} %get-tuple-element.137.refs_4_), channel_id=1, source_target_pairs={{0,1},{1,0},{2,3},{3,2},{4,5},{5,4},{6,7},{7,6},{8,9},{9,8},{10,11... | collective-permute-start | bytes 1769480 | tf_op jit(solution)/shard_map/ppermute | solution.py:164
  3.7 11.3 %collective-permute-start = (bf16[576,512]{1,0:T(8,128)(2,1)S(1)}, bf16[576,512]{1,0:T(8,128)(2,1)}, u32[]{:S(2)}, u32[]{:S(2)}) collective-permute-start(bf16[576,512]{1,0:T(8,128)(2,1)S(1)} %get-tuple-element.138.refs_3_), channel_id=1, source_target_pairs={{0,1},{1,0},{2,3},{3,2},{4,5},{5,4},{6,7},{7,6},{8,9},{9,8},{10,11... | collective-permute-start | bytes 1769480 | tf_op jit(solution)/shard_map/ppermute | solution.py:164
  3.8 19.0 %collective-permute-start.3 = (bf16[576,512]{1,0:T(8,128)(2,1)S(1)}, bf16[576,512]{1,0:T(8,128)(2,1)S(1)}, u32[]{:S(2)}, u32[]{:S(2)}) collective-permute-start(bf16[576,512]{1,0:T(8,128)(2,1)S(1)} %get-tuple-element.137.refs_4_), channel_id=1, source_target_pairs={{0,6},{1,7},{2,0},{3,1},{4,2},{5,3},{6,4},{7,5},{8,14},{9,15},{10,... | collective-permute-start | bytes 1769480 | tf_op jit(solution)/shard_map/ppermute | solution.py:161
  7.4 15.4 %collective-permute-start.2 = (bf16[576,512]{1,0:T(8,128)(2,1)S(1)}, bf16[576,512]{1,0:T(8,128)(2,1)S(1)}, u32[]{:S(2)}, u32[]{:S(2)}) collective-permute-start(bf16[576,512]{1,0:T(8,128)(2,1)S(1)} %get-tuple-element.138.refs_3_), channel_id=1, source_target_pairs={{0,2},{1,3},{2,4},{3,5},{4,6},{5,7},{6,0},{7,1},{8,10},{9,11},{10,... | collective-permute-start | bytes 1769480 | tf_op jit(solution)/shard_map/ppermute | solution.py:161
  15.0 9.3 %copy-start.4 = (bf16[512,512]{1,0:T(8,128)(2,1)S(1)}, bf16[512,512]{1,0:T(8,128)(2,1)}, u32[]{:S(2)}) copy-start(bf16[512,512]{1,0:T(8,128)(2,1)} %copy-done.3) | copy-start | bytes 1572868
  15.0 9.3 %copy-start.2 = (bf16[512,512]{1,0:T(8,128)(2,1)S(1)}, bf16[512,512]{1,0:T(8,128)(2,1)}, u32[]{:S(2)}) copy-start(bf16[512,512]{1,0:T(8,128)(2,1)} %copy-done.1) | copy-start | bytes 1572868
  22.8 10.7 %collective-permute-start.4 = (bf16[576,512]{1,0:T(8,128)(2,1)S(1)}, bf16[576,512]{1,0:T(8,128)(2,1)S(1)}, u32[]{:S(2)}, u32[]{:S(2)}) collective-permute-start(bf16[576,512]{1,0:T(8,128)(2,1)S(1)} %collective-permute-done.2.refs_4_), channel_id=1, source_target_pairs={{0,1},{1,0},{2,3},{3,2},{4,5},{5,4},{6,7},{7,6},{8,9},{9,8},{10,11... | collective-permute-start | bytes 1769480 | tf_op jit(solution)/shard_map/ppermute | solution.py:164
  24.4 9.1 %collective-permute-start.5 = (bf16[576,512]{1,0:T(8,128)(2,1)S(1)}, bf16[576,512]{1,0:T(8,128)(2,1)S(1)}, u32[]{:S(2)}, u32[]{:S(2)}) collective-permute-start(bf16[576,512]{1,0:T(8,128)(2,1)S(1)} %collective-permute-done.3.refs_5_), channel_id=1, source_target_pairs={{0,1},{1,0},{2,3},{3,2},{4,5},{5,4},{6,7},{7,6},{8,9},{9,8},{10,11... | collective-permute-start | bytes 1769480 | tf_op jit(solution)/shard_map/ppermute | solution.py:164
  24.4 15.6 %collective-permute-start.6 = (bf16[512,512]{1,0:T(8,128)(2,1)S(1)}, bf16[512,512]{1,0:T(8,128)(2,1)S(1)}, u32[]{:S(2)}, u32[]{:S(2)}) collective-permute-start(bf16[512,512]{1,0:T(8,128)(2,1)S(1)} %copy-done.4), channel_id=1, source_target_pairs={{0,2},{1,3},{2,4},{3,5},{4,6},{5,7},{6,0},{7,1},{8,10},{9,11},{10,... | collective-permute-start | bytes 1572872 | tf_op jit(solution)/shard_map/ppermute | solution.py:161
  24.4 15.6 %collective-permute-start.7 = (bf16[512,512]{1,0:T(8,128)(2,1)S(1)}, bf16[512,512]{1,0:T(8,128)(2,1)S(1)}, u32[]{:S(2)}, u32[]{:S(2)}) collective-permute-start(bf16[512,512]{1,0:T(8,128)(2,1)S(1)} %copy-done.2), channel_id=1, source_target_pairs={{0,6},{1,7},{2,0},{3,1},{4,2},{5,3},{6,4},{7,5},{8,14},{9,15},{10,... | collective-permute-start | bytes 1572872 | tf_op jit(solution)/shard_map/ppermute | solution.py:161
  40.0 10.2 %collective-permute-start.8 = (bf16[512,512]{1,0:T(8,128)(2,1)S(1)}, bf16[512,512]{1,0:T(8,128)(2,1)S(1)}, u32[]{:S(2)}, u32[]{:S(2)}) collective-permute-start(bf16[512,512]{1,0:T(8,128)(2,1)S(1)} %collective-permute-done.6.refs_4_), channel_id=1, source_target_pairs={{0,1},{1,0},{2,3},{3,2},{4,5},{5,4},{6,7},{7,6},{8,9},{9,8},{10,11... | collective-permute-start | bytes 1572872 | tf_op jit(solution)/shard_map/ppermute | solution.py:164
  41.1 9.1 %collective-permute-start.9 = (bf16[512,512]{1,0:T(8,128)(2,1)S(1)}, bf16[512,512]{1,0:T(8,128)(2,1)S(1)}, u32[]{:S(2)}, u32[]{:S(2)}) collective-permute-start(bf16[512,512]{1,0:T(8,128)(2,1)S(1)} %collective-permute-done.7.refs_5_), channel_id=1, source_target_pairs={{0,1},{1,0},{2,3},{3,2},{4,5},{5,4},{6,7},{7,6},{8,9},{9,8},{10,11... | collective-permute-start | bytes 1572872 | tf_op jit(solution)/shard_map/ppermute | solution.py:164
  41.2 15.7 %collective-permute-start.10 = (bf16[576,512]{1,0:T(8,128)(2,1)S(1)}, bf16[576,512]{1,0:T(8,128)(2,1)S(1)}, u32[]{:S(2)}, u32[]{:S(2)}) collective-permute-start(bf16[576,512]{1,0:T(8,128)(2,1)S(1)} %collective-permute-done.2.refs_4_), channel_id=1, source_target_pairs={{0,2},{1,3},{2,4},{3,5},{4,6},{5,7},{6,0},{7,1},{8,10},{9,11},{10,... | collective-permute-start | bytes 1769480 | tf_op jit(solution)/shard_map/ppermute | solution.py:161
  41.2 15.7 %collective-permute-start.11 = (bf16[576,512]{1,0:T(8,128)(2,1)S(1)}, bf16[576,512]{1,0:T(8,128)(2,1)S(1)}, u32[]{:S(2)}, u32[]{:S(2)}) collective-permute-start(bf16[576,512]{1,0:T(8,128)(2,1)S(1)} %collective-permute-done.3.refs_5_), channel_id=1, source_target_pairs={{0,6},{1,7},{2,0},{3,1},{4,2},{5,3},{6,4},{7,5},{8,14},{9,15},{10,... | collective-permute-start | bytes 1769480 | tf_op jit(solution)/shard_map/ppermute | solution.py:161
  56.9 7.7 %collective-permute-start.12 = (bf16[576,512]{1,0:T(8,128)(2,1)S(1)}, bf16[576,512]{1,0:T(8,128)(2,1)S(1)}, u32[]{:S(2)}, u32[]{:S(2)}) collective-permute-start(bf16[576,512]{1,0:T(8,128)(2,1)S(1)} %collective-permute-done.10.refs_4_), channel_id=1, source_target_pairs={{0,1},{1,0},{2,3},{3,2},{4,5},{5,4},{6,7},{7,6},{8,9},{9,8},{10,11... | collective-permute-start | bytes 1769480 | tf_op jit(solution)/shard_map/ppermute | solution.py:164
  58.2 6.5 %collective-permute-start.13 = (bf16[576,512]{1,0:T(8,128)(2,1)S(1)}, bf16[576,512]{1,0:T(8,128)(2,1)S(1)}, u32[]{:S(2)}, u32[]{:S(2)}) collective-permute-start(bf16[576,512]{1,0:T(8,128)(2,1)S(1)} %collective-permute-done.11.refs_5_), channel_id=1, source_target_pairs={{0,1},{1,0},{2,3},{3,2},{4,5},{5,4},{6,7},{7,6},{8,9},{9,8},{10,11... | collective-permute-start | bytes 1769480 | tf_op jit(solution)/shard_map/ppermute | solution.py:164
  58.2 6.5 %copy-start = (f32[64,512]{1,0:T(8,128)S(1)}, f32[64,512]{1,0:T(8,128)}, u32[]{:S(2)}) copy-start(f32[64,512]{1,0:T(8,128)} %refs_10_.1) | copy-start | bytes 393220

commit v5 on v3

--- a/solution.py
+++ b/solution.py
@@ -9,6 +9,7 @@
 
 EMA_DECAY = 0.9
 SPLIT = 4
+SUB = 4
 AHEAD = 3
 GRANT = 12 << 20
 
@@ -34,7 +35,7 @@
 
 
 def _gather_kernel(n, grad, lroot, right, rroot, rbuf, xacc, lbuf, gbuf, gt, rr,
-                   own_sem, r_sem, rr_sem, recv, send_p, send_m, send_d,
+                   own_sem, r_sem, rr_sem, recv, recv_sub, send_p, send_m, send_d,
                    l_own, l_recv, l_send):
     me = lax.axis_index("tensor")
     mate = me + 1 - 2 * (me % 2)
@@ -65,6 +66,12 @@
             src_ref=gbuf.at[sl], dst_ref=gbuf.at[sl], send_sem=sem, recv_sem=recv.at[sl],
             device_id={"tensor": dev}, device_id_type=MESH)
 
+    def part(sl, r, sem, group, dev):
+        at = gbuf.at[sl, pl.ds(r * (rows // SUB), rows // SUB)]
+        return pltpu.make_async_remote_copy(
+            src_ref=at, dst_ref=at, send_sem=sem, recv_sem=recv_sub.at[group, r],
+            device_id={"tensor": dev}, device_id_type=MESH)
+
     def lpart(owner, first, count, s_idx, r_idx, dev):
         at = pl.ds(pl.multiple_of(owner * nl + first, hl), count)
         return pltpu.make_async_remote_copy(
@@ -89,20 +96,21 @@
         pl.semaphore_signal(barrier, inc=1, device_id={"tensor": dev}, device_id_type=MESH)
     pl.semaphore_wait(barrier, 3)
 
-    for c in own:
-        c.wait()
-    lown.wait()
-    sent = []
+    landed = set()
     for s in range(SPLIT):
-        sent.append(piece(me * SPLIT + s, send_p.at[s], plus))
-        sent.append(piece(me * SPLIT + (s + 2) % SPLIT, send_m.at[s], minus))
-        sent.append(piece(me * SPLIT + s, send_d.at[s], mate))
+        for q in (s, (s + 2) % SPLIT):
+            if q not in landed:
+                own[q].wait()
+                landed.add(q)
+        piece(me * SPLIT + s, send_p.at[s], plus).start()
+        piece(me * SPLIT + (s + 2) % SPLIT, send_m.at[s], minus).start()
         if s == 0:
-            sent.append(lpart(me, 0, nl, 0, 0, plus))
-            sent.append(lpart(me, 0, nl, 1, 1, minus))
-            sent.append(lpart(me, 0, nl, 2, 4, mate))
-    for c in sent:
-        c.start()
+            lown.wait()
+            lpart(me, 0, nl, 0, 0, plus).start()
+            lpart(me, 0, nl, 1, 1, minus).start()
+    for s in range(SPLIT):
+        piece(me * SPLIT + s, send_d.at[s], mate).start()
+    lpart(me, 0, nl, 2, 4, mate).start()
     for t in range(AHEAD):
         loads(t, 4 * t)
     for q in range(SPLIT):
@@ -141,14 +149,17 @@
         def _():
             a, b = slot(t, 0, 0), slot(t, 0, 1)
             arrived(a)
+            piece(a, send_d.at[SPLIT + 2 * s], mate).start()
+
+            @pl.when(s == 0)
+            def _():
+                piece(a, send_p.at[SPLIT], plus).start()
             arrived(b)
-
-            @pl.when(s < 2)
+            piece(b, send_d.at[SPLIT + 2 * s + 1], mate).start()
+
+            @pl.when(s == 0)
             def _():
-                piece(a, send_p.at[SPLIT + s], plus).start()
-                piece(b, send_m.at[SPLIT + s], minus).start()
-            piece(a, send_d.at[SPLIT + 2 * s], mate).start()
-            piece(b, send_d.at[SPLIT + 2 * s + 1], mate).start()
+                piece(b, send_m.at[SPLIT], minus).start()
 
             @pl.when(s == 1)
             def _():
@@ -156,15 +167,22 @@
                 lpart(plus, 0, nl, 1, 1, minus).wait_recv()
                 lpart(minus, 0, hl, 3, 2, plus).start()
                 lpart(plus, hl, hl, 4, 3, minus).start()
+                for r in range(SUB):
+                    part(a, r, send_p.at[SPLIT + 1 + r], 0, plus).start()
+                    part(b, r, send_m.at[SPLIT + 1 + r], 1, minus).start()
                 lpart(minus, 0, nl, 5, 5, mate).start()
                 lpart(plus, 0, nl, 6, 6, mate).start()
 
-            @pl.when(s == steps - 1)
-            def _():
-                far = ring(me + 4)
-                lpart(far, 0, hl, 3, 2, plus).wait_recv()
-                lpart(far, hl, hl, 4, 3, minus).wait_recv()
-                lpart(far, 0, nl, 7, 7, mate).start()
+    def take_last(t):
+        far = ring(me + 4)
+        lpart(far, 0, hl, 3, 2, plus).wait_recv()
+        lpart(far, hl, hl, 4, 3, minus).wait_recv()
+        lpart(far, 0, nl, 7, 7, mate).start()
+        for r in range(SUB):
+            for i in range(2):
+                sl = slot(t, 0, i)
+                part(sl, r, send_d.at[0], i, mate).wait_recv()
+                part(sl, r, send_d.at[SPLIT + 2 * (steps - 1) + i * SUB + r], 2 + i, mate).start()
 
     def take_mate(t):
         @pl.when(t >= 2)
@@ -187,18 +205,26 @@
     lax.fori_loop(0, steps + 1, step, 0)
     last = steps + 1
     k0 = 4 * (last % AHEAD)
-    take(last)
+    take_last(last)
     ready(last, 0, k0)
-    take_mate(last)
+    for r in range(SUB):
+        for i in range(2):
+            part(slot(last, 1, i), r, send_d.at[0], 2 + i, mate).wait_recv()
     ready(last, 1, k0 + 2)
 
     for r_idx in (4, 5, 6, 7):
         lpart(me, 0, nl, 2, r_idx, mate).wait_recv()
-    for s in range(steps):
+    for s in range(SPLIT + 1):
         piece(me * SPLIT, send_p.at[s], plus).wait_send()
         piece(me * SPLIT, send_m.at[s], minus).wait_send()
-    for s in range(SPLIT + 2 * steps):
+    for r in range(SUB):
+        part(me * SPLIT, r, send_p.at[SPLIT + 1 + r], 0, plus).wait_send()
+        part(me * SPLIT, r, send_m.at[SPLIT + 1 + r], 1, minus).wait_send()
+    whole = SPLIT + 2 * (steps - 1)
+    for s in range(whole):
         piece(me * SPLIT, send_d.at[s], mate).wait_send()
+    for s in range(2 * SUB):
+        part(me * SPLIT, 0, send_d.at[whole + s], 2, mate).wait_send()
     for k in range(8):
         lpart(me, 0, hl if k in (3, 4) else nl, k, 0, mate).wait_send()
 
@@ -206,7 +232,6 @@
 def _write_kernel(n, rbuf, xacc, lbuf, gbuf, gt, rr, left, r_out, l_out, d_out,
                   tail, xs, d_buf, l_buf, r_sem, sem):
     me = lax.axis_index("tensor")
-    mate = me + 1 - 2 * (me % 2)
     width = gbuf.shape[2]
     cols, nl = d_buf.shape[1], left.shape[0]
     last = 7
@@ -215,27 +240,38 @@
     def span(sl):
         return pl.ds(pl.multiple_of(sl * width, width), width)
 
+    left_copy = pltpu.make_async_copy(left, l_buf, sem.at[0])
+    left_copy.start()
+    copies = []
+
+    def write(src, dst):
+        copies.append(pltpu.make_async_copy(src, dst, r_sem.at[len(copies)]))
+        copies[-1].start()
+
+    chips = n // 2
+    far = me // 2 + chips // 2
+    tall, wide = cols // 4, 2 * cols
+    for c in range(1, chips):
+        at = pl.ds(pl.multiple_of(lax.rem(far + c, chips) * wide, wide), wide)
+        for p in range(4):
+            block = (pl.ds(p * tall, tall), at)
+            write(rbuf.at[block], r_out.at[block])
+    for u in range(2):
+        for i in range(2):
+            at = span(_slot(n, me, last - 1, u, i))
+            write(rbuf.at[:, at], r_out.at[:, at])
     tails = [_slot(n, me, last, u, i) for u in range(2) for i in range(2)]
-    copies = []
-    for t in range(last):
-        for u in range(2):
-            for i in range(2):
-                at = span(_slot(n, me, t, u, i))
-                copies.append(pltpu.make_async_copy(rbuf.at[:, at], r_out.at[:, at], r_sem.at[len(copies)]))
-                copies[-1].start(priority=len(copies) % 2)
     for k, sl in enumerate(tails):
         tail[k] = EMA_DECAY * rbuf[:, span(sl)] + (1.0 - EMA_DECAY) * jnp.dot(
             gt[...], gbuf[sl], preferred_element_type=jnp.float32)
-        copies.append(pltpu.make_async_copy(tail.at[k], r_out.at[:, span(sl)], r_sem.at[len(copies)]))
-        copies[-1].start(priority=len(copies) % 2)
+        write(tail.at[k], r_out.at[:, span(sl)])
     xs[...] = xacc[...] + _nt(rr[k0], gbuf[tails[0]]) + _nt(rr[k0 + 1], gbuf[tails[1]])
     xs[...] += _nt(rr[k0 + 2], gbuf[tails[2]]) + _nt(rr[k0 + 3], gbuf[tails[3]])
-    l_buf[...] = EMA_DECAY * left[...] + (1.0 - EMA_DECAY) * xs[pl.ds(cols, nl), :]
     d_buf[...] = _nt(lbuf[...], xs[pl.ds(0, cols), :].astype(jnp.bfloat16))
-    copies.append(pltpu.make_async_copy(l_buf, l_out, sem.at[0]))
-    copies[-1].start(priority=len(copies) % 2)
-    copies.append(pltpu.make_async_copy(d_buf, d_out, sem.at[1]))
-    copies[-1].start(priority=len(copies) % 2)
+    write(d_buf, d_out)
+    left_copy.wait()
+    l_buf[...] = EMA_DECAY * l_buf[...] + (1.0 - EMA_DECAY) * xs[pl.ds(cols, nl), :]
+    write(l_buf, l_out)
     for c in copies:
         c.wait()
 
@@ -260,7 +296,7 @@
             out_specs=(VMEM,) * 6,
             scratch_shapes=[
                 dma((SPLIT,)), dma((n * SPLIT,)), dma((4 * AHEAD,)), dma((n * SPLIT,)),
-                dma((6,)), dma((6,)), dma((16,)),
+                dma((4, SUB)), dma((SPLIT + 1 + SUB,)), dma((SPLIT + 1 + SUB,)), dma((SPLIT + 10 + 2 * SUB,)),
                 dma(()), dma((8,)), dma((8,)),
             ],
             compiler_params=pltpu.CompilerParams(collective_id=0, has_side_effects=True, vmem_limit_bytes=GRANT),
@@ -269,10 +305,10 @@
             functools.partial(_write_kernel, n),
             out_shape=(jax.ShapeDtypeStruct(right.shape, f32), jax.ShapeDtypeStruct((nl, rows), f32),
                        jax.ShapeDtypeStruct((rows, cols), f32)),
-            in_specs=[VMEM] * 7,
+            in_specs=[VMEM] * 6 + [ANY],
             out_specs=(ANY,) * 3,
             scratch_shapes=[pltpu.VMEM((4, cols, width), f32), pltpu.VMEM((cols + nl, rows), f32),
-                            pltpu.VMEM((rows, cols), f32), pltpu.VMEM((nl, rows), f32), dma((n * SPLIT,)), dma((2,))],
+                            pltpu.VMEM((rows, cols), f32), pltpu.VMEM((nl, rows), f32), dma((22,)), dma((1,))],
             compiler_params=pltpu.CompilerParams(vmem_limit_bytes=GRANT),
         )(*[pltpu.with_memory_space_constraint(v, pltpu.VMEM) for v in held], left)
         return l, r, d

time: 58.4 us -> 57.1 us (0.978)
  Pallas kernels: 57.6 us -> 56.4 us
    pallas_call x1, Pallas kernels: 12.9 us -> 11.8 us  [local_step(): pl.pallas_call(functools.partial(_write_kernel, n), out_shape=(jax.ShapeD...]
where the time goes in v5:
time: 57.1 us; the launch traced here: 57 us
  Pallas kernels  56.4 us (99%)
  between operations  0.64 us (1%)
    pallas_call x1, Pallas kernels, local_step(): pl.pallas_call(functools.partial(_gather_kernel, n), out_shape=(pltpu.VME...  44.6 us
    pallas_call x1, Pallas kernels, local_step(): pl.pallas_call(functools.partial(_write_kernel, n), out_shape=(jax.ShapeD...  11.8 us

profile of v5, /device:TPU:113, one launch (start us, length us, event | category | flops | bytes accessed | tf_op | source)
XLA Modules:
  0.0 57.0 jit_solution(14105190816373063455)
XLA Ops:
  0.6 44.6 %shard_map.76 = (f32[1024,8192]{1,0:T(8,128)S(1)}, f32[1088,512]{1,0:T(8,128)S(1)}, bf16[512,512]{1,0:T(8,128)(2,1)S(1)}, bf16[32,512,256]{2,1,0:T(8,128)(2,1)S(...) custom-call(bf16[512,1024]{1,0:T(8,128)(2,1)} %grad.1, bf16[64,512]{1,0:T(8,128)(2,1)} %lroot.1, ...), custom_call_target="tpu_custom_call" | custom-call | tf_op jit(solution)/shard_map/pallas_call | solution.py:290
  45.2 11.8 %shard_map.77 = (f32[1024,8192]{1,0:T(8,128)}, f32[64,512]{1,0:T(8,128)}, f32[512,1024]{1,0:T(8,128)}) custom-call(f32[1024,8192]{1,0:T(8,128)S(1)} %get-tuple-element.12.rbuf, f32[1088,512]{1,0:T(8,128)S(1)} %get-tuple-element.13.xacc, bf16[512,512]{1,0:T(8,128)(2,1)S(1)} %get-tuple-element.14.lbuf, bf16[32,512,256]{2,1,0:T(8,128)(2,1)S(1)} %get-tuple-element.15.gbuf, ...), custom_call_target="tpu_custom_call" | custom-call | tf_op jit(solution)/shard_map/pallas_call | solution.py:304

commit v6 on v5

--- a/solution.py
+++ b/solution.py
@@ -9,7 +9,7 @@
 
 EMA_DECAY = 0.9
 SPLIT = 4
-SUB = 4
+SUB = 8
 AHEAD = 3
 GRANT = 12 << 20
 
@@ -79,10 +79,10 @@
             device_id={"tensor": dev}, device_id_type=MESH)
 
     own = [own_copy(q) for q in range(SPLIT)]
-    for c in own:
-        c.start()
     lown = pltpu.make_async_copy(lroot, lbuf.at[pl.ds(pl.multiple_of(me * nl, nl), nl)], l_own)
     lown.start()
+    for q in (0, 2, 1, 3):
+        own[q].start()
 
     def loads(t, k0):
         for u in range(2):
@@ -97,6 +97,9 @@
     pl.semaphore_wait(barrier, 3)
 
     landed = set()
+    lown.wait()
+    lpart(me, 0, nl, 0, 0, plus).start()
+    lpart(me, 0, nl, 1, 1, minus).start()
     for s in range(SPLIT):
         for q in (s, (s + 2) % SPLIT):
             if q not in landed:
@@ -104,10 +107,6 @@
                 landed.add(q)
         piece(me * SPLIT + s, send_p.at[s], plus).start()
         piece(me * SPLIT + (s + 2) % SPLIT, send_m.at[s], minus).start()
-        if s == 0:
-            lown.wait()
-            lpart(me, 0, nl, 0, 0, plus).start()
-            lpart(me, 0, nl, 1, 1, minus).start()
     for s in range(SPLIT):
         piece(me * SPLIT + s, send_d.at[s], mate).start()
     lpart(me, 0, nl, 2, 4, mate).start()
@@ -250,10 +249,10 @@
 
     chips = n // 2
     far = me // 2 + chips // 2
-    tall, wide = cols // 4, 2 * cols
+    tall, wide = cols // 2, 2 * cols
     for c in range(1, chips):
         at = pl.ds(pl.multiple_of(lax.rem(far + c, chips) * wide, wide), wide)
-        for p in range(4):
+        for p in range(2):
             block = (pl.ds(p * tall, tall), at)
             write(rbuf.at[block], r_out.at[block])
     for u in range(2):

time: 57.1 us -> 57.3 us (level)
  no operation moved by 1% of the time
where the time goes in v6:
time: 57.3 us; the launch traced here: 57.2 us
  Pallas kernels  56.6 us (99%)
  between operations  0.64 us (1%)
    pallas_call x1, Pallas kernels, local_step(): pl.pallas_call(functools.partial(_gather_kernel, n), out_shape=(pltpu.VME...  44.8 us
    pallas_call x1, Pallas kernels, local_step(): pl.pallas_call(functools.partial(_write_kernel, n), out_shape=(jax.ShapeD...  11.8 us

profile of v6, /device:TPU:113, one launch (start us, length us, event | category | flops | bytes accessed | tf_op | source)
XLA Modules:
  0.0 57.2 jit_solution(2634576247352732377)
XLA Ops:
  0.6 44.8 %shard_map.76 = (f32[1024,8192]{1,0:T(8,128)S(1)}, f32[1088,512]{1,0:T(8,128)S(1)}, bf16[512,512]{1,0:T(8,128)(2,1)S(1)}, bf16[32,512,256]{2,1,0:T(8,128)(2,1)S(...) custom-call(bf16[512,1024]{1,0:T(8,128)(2,1)} %grad.1, bf16[64,512]{1,0:T(8,128)(2,1)} %lroot.1, ...), custom_call_target="tpu_custom_call" | custom-call | tf_op jit(solution)/shard_map/pallas_call | solution.py:289
  45.4 11.8 %shard_map.77 = (f32[1024,8192]{1,0:T(8,128)}, f32[64,512]{1,0:T(8,128)}, f32[512,1024]{1,0:T(8,128)}) custom-call(f32[1024,8192]{1,0:T(8,128)S(1)} %get-tuple-element.12.rbuf, f32[1088,512]{1,0:T(8,128)S(1)} %get-tuple-element.13.xacc, bf16[512,512]{1,0:T(8,128)(2,1)S(1)} %get-tuple-element.14.lbuf, bf16[32,512,256]{2,1,0:T(8,128)(2,1)S(1)} %get-tuple-element.15.gbuf, ...), custom_call_target="tpu_custom_call" | custom-call | tf_op jit(solution)/shard_map/pallas_call | solution.py:303

commit v7 on v5

--- a/solution.py
+++ b/solution.py
@@ -9,7 +9,7 @@
 
 EMA_DECAY = 0.9
 SPLIT = 4
-SUB = 4
+SUB = 2
 AHEAD = 3
 GRANT = 12 << 20
 
@@ -66,6 +66,12 @@
             src_ref=gbuf.at[sl], dst_ref=gbuf.at[sl], send_sem=sem, recv_sem=recv.at[sl],
             device_id={"tensor": dev}, device_id_type=MESH)
 
+    def pair(sl, sem, dev):
+        at = gbuf.at[pl.ds(sl, 2)]
+        return pltpu.make_async_remote_copy(
+            src_ref=at, dst_ref=at, send_sem=sem, recv_sem=recv.at[sl],
+            device_id={"tensor": dev}, device_id_type=MESH)
+
     def part(sl, r, sem, group, dev):
         at = gbuf.at[sl, pl.ds(r * (rows // SUB), rows // SUB)]
         return pltpu.make_async_remote_copy(
@@ -96,20 +102,20 @@
         pl.semaphore_signal(barrier, inc=1, device_id={"tensor": dev}, device_id_type=MESH)
     pl.semaphore_wait(barrier, 3)
 
-    landed = set()
-    for s in range(SPLIT):
-        for q in (s, (s + 2) % SPLIT):
-            if q not in landed:
-                own[q].wait()
-                landed.add(q)
-        piece(me * SPLIT + s, send_p.at[s], plus).start()
-        piece(me * SPLIT + (s + 2) % SPLIT, send_m.at[s], minus).start()
-        if s == 0:
-            lown.wait()
-            lpart(me, 0, nl, 0, 0, plus).start()
-            lpart(me, 0, nl, 1, 1, minus).start()
-    for s in range(SPLIT):
-        piece(me * SPLIT + s, send_d.at[s], mate).start()
+    base = me * SPLIT
+    for q in (0, 1):
+        own[q].wait()
+    pair(base, send_p.at[0], plus).start()
+    for q in (2, 3):
+        own[q].wait()
+    pair(base + 2, send_m.at[0], minus).start()
+    lown.wait()
+    lpart(me, 0, nl, 0, 0, plus).start()
+    lpart(me, 0, nl, 1, 1, minus).start()
+    pair(base + 2, send_p.at[1], plus).start()
+    pair(base, send_m.at[1], minus).start()
+    pair(base, send_d.at[0], mate).start()
+    pair(base + 2, send_d.at[1], mate).start()
     lpart(me, 0, nl, 2, 4, mate).start()
     for t in range(AHEAD):
         loads(t, 4 * t)
@@ -137,29 +143,34 @@
     def arrived(sl):
         piece(sl, send_d.at[0], mate).wait_recv()
 
+    def pair_arrived(sl):
+        pair(sl, send_d.at[0], mate).wait_recv()
+
     def take(t):
         s = t - 2
 
         @pl.when(t == 1)
         def _():
-            for q in range(SPLIT):
-                arrived(mate * SPLIT + q)
+            for q in (0, 2):
+                pair_arrived(mate * SPLIT + q)
 
         @pl.when(t >= 2)
         def _():
             a, b = slot(t, 0, 0), slot(t, 0, 1)
-            arrived(a)
-            piece(a, send_d.at[SPLIT + 2 * s], mate).start()
-
-            @pl.when(s == 0)
+
+            @pl.when((s == 0) | (s == 2))
             def _():
-                piece(a, send_p.at[SPLIT], plus).start()
-            arrived(b)
-            piece(b, send_d.at[SPLIT + 2 * s + 1], mate).start()
-
-            @pl.when(s == 0)
+                pair_arrived(a)
+                pair(a, send_d.at[2 + s], mate).start()
+                pair_arrived(b)
+                pair(b, send_d.at[3 + s], mate).start()
+
+            @pl.when(s == 4)
             def _():
-                piece(b, send_m.at[SPLIT], minus).start()
+                arrived(a)
+                piece(a, send_d.at[6], mate).start()
+                arrived(b)
+                piece(b, send_d.at[7], mate).start()
 
             @pl.when(s == 1)
             def _():
@@ -167,9 +178,11 @@
                 lpart(plus, 0, nl, 1, 1, minus).wait_recv()
                 lpart(minus, 0, hl, 3, 2, plus).start()
                 lpart(plus, hl, hl, 4, 3, minus).start()
+                piece(a - 1, send_p.at[2], plus).start()
+                piece(b - 1, send_m.at[2], minus).start()
                 for r in range(SUB):
-                    part(a, r, send_p.at[SPLIT + 1 + r], 0, plus).start()
-                    part(b, r, send_m.at[SPLIT + 1 + r], 1, minus).start()
+                    part(a, r, send_p.at[3 + r], 0, plus).start()
+                    part(b, r, send_m.at[3 + r], 1, minus).start()
                 lpart(minus, 0, nl, 5, 5, mate).start()
                 lpart(plus, 0, nl, 6, 6, mate).start()
 
@@ -182,10 +195,17 @@
             for i in range(2):
                 sl = slot(t, 0, i)
                 part(sl, r, send_d.at[0], i, mate).wait_recv()
-                part(sl, r, send_d.at[SPLIT + 2 * (steps - 1) + i * SUB + r], 2 + i, mate).start()
+                part(sl, r, send_d.at[8 + i * SUB + r], 2 + i, mate).start()
 
     def take_mate(t):
-        @pl.when(t >= 2)
+        s = t - 2
+
+        @pl.when((s == 0) | (s == 2))
+        def _():
+            pair_arrived(slot(t, 1, 0))
+            pair_arrived(slot(t, 1, 1))
+
+        @pl.when(s == 4)
         def _():
             arrived(slot(t, 1, 0))
             arrived(slot(t, 1, 1))
@@ -214,17 +234,20 @@
 
     for r_idx in (4, 5, 6, 7):
         lpart(me, 0, nl, 2, r_idx, mate).wait_recv()
-    for s in range(SPLIT + 1):
-        piece(me * SPLIT, send_p.at[s], plus).wait_send()
-        piece(me * SPLIT, send_m.at[s], minus).wait_send()
+    for s in range(2):
+        pair(base, send_p.at[s], plus).wait_send()
+        pair(base, send_m.at[s], minus).wait_send()
+    piece(base, send_p.at[2], plus).wait_send()
+    piece(base, send_m.at[2], minus).wait_send()
     for r in range(SUB):
-        part(me * SPLIT, r, send_p.at[SPLIT + 1 + r], 0, plus).wait_send()
-        part(me * SPLIT, r, send_m.at[SPLIT + 1 + r], 1, minus).wait_send()
-    whole = SPLIT + 2 * (steps - 1)
-    for s in range(whole):
-        piece(me * SPLIT, send_d.at[s], mate).wait_send()
+        part(base, r, send_p.at[3 + r], 0, plus).wait_send()
+        part(base, r, send_m.at[3 + r], 1, minus).wait_send()
+    for s in range(6):
+        pair(base, send_d.at[s], mate).wait_send()
+    for s in (6, 7):
+        piece(base, send_d.at[s], mate).wait_send()
     for s in range(2 * SUB):
-        part(me * SPLIT, 0, send_d.at[whole + s], 2, mate).wait_send()
+        part(base, 0, send_d.at[8 + s], 2, mate).wait_send()
     for k in range(8):
         lpart(me, 0, hl if k in (3, 4) else nl, k, 0, mate).wait_send()
 
@@ -296,7 +319,7 @@
             out_specs=(VMEM,) * 6,
             scratch_shapes=[
                 dma((SPLIT,)), dma((n * SPLIT,)), dma((4 * AHEAD,)), dma((n * SPLIT,)),
-                dma((4, SUB)), dma((SPLIT + 1 + SUB,)), dma((SPLIT + 1 + SUB,)), dma((SPLIT + 10 + 2 * SUB,)),
+                dma((4, SUB)), dma((3 + SUB,)), dma((3 + SUB,)), dma((8 + 2 * SUB,)),
                 dma(()), dma((8,)), dma((8,)),
             ],
             compiler_params=pltpu.CompilerParams(collective_id=0, has_side_effects=True, vmem_limit_bytes=GRANT),

time: 57.1 us -> 57 us (level)
  no operation moved by 1% of the time
where the time goes in v7:
time: 57 us; the launch traced here: 56.9 us
  Pallas kernels  56.2 us (99%)
  between operations  0.64 us (1%)
    pallas_call x1, Pallas kernels, local_step(): pl.pallas_call(functools.partial(_gather_kernel, n), out_shape=(pltpu.VME...  44.4 us
    pallas_call x1, Pallas kernels, local_step(): pl.pallas_call(functools.partial(_write_kernel, n), out_shape=(jax.ShapeD...  11.8 us

profile of v7, /device:TPU:113, one launch (start us, length us, event | category | flops | bytes accessed | tf_op | source)
XLA Modules:
  0.0 56.9 jit_solution(6842378981712843478)
XLA Ops:
  0.6 44.4 %shard_map.76 = (f32[1024,8192]{1,0:T(8,128)S(1)}, f32[1088,512]{1,0:T(8,128)S(1)}, bf16[512,512]{1,0:T(8,128)(2,1)S(1)}, bf16[32,512,256]{2,1,0:T(8,128)(2,1)S(...) custom-call(bf16[512,1024]{1,0:T(8,128)(2,1)} %grad.1, bf16[64,512]{1,0:T(8,128)(2,1)} %lroot.1, ...), custom_call_target="tpu_custom_call" | custom-call | tf_op jit(solution)/shard_map/pallas_call | solution.py:313
  45.1 11.8 %shard_map.77 = (f32[1024,8192]{1,0:T(8,128)}, f32[64,512]{1,0:T(8,128)}, f32[512,1024]{1,0:T(8,128)}) custom-call(f32[1024,8192]{1,0:T(8,128)S(1)} %get-tuple-element.12.rbuf, f32[1088,512]{1,0:T(8,128)S(1)} %get-tuple-element.13.xacc, bf16[512,512]{1,0:T(8,128)(2,1)S(1)} %get-tuple-element.14.lbuf, bf16[32,512,256]{2,1,0:T(8,128)(2,1)S(1)} %get-tuple-element.15.gbuf, ...), custom_call_target="tpu_custom_call" | custom-call | tf_op jit(solution)/shard_map/pallas_call | solution.py:327

commit v8 on v7

--- a/solution.py
+++ b/solution.py
@@ -73,7 +73,8 @@
             device_id={"tensor": dev}, device_id_type=MESH)
 
     def part(sl, r, sem, group, dev):
-        at = gbuf.at[sl, pl.ds(r * (rows // SUB), rows // SUB)]
+        first = rows * 3 // 4
+        at = gbuf.at[sl, pl.ds(0, first) if r == 0 else pl.ds(first, rows - first)]
         return pltpu.make_async_remote_copy(
             src_ref=at, dst_ref=at, send_sem=sem, recv_sem=recv_sub.at[group, r],
             device_id={"tensor": dev}, device_id_type=MESH)
@@ -246,8 +247,9 @@
         pair(base, send_d.at[s], mate).wait_send()
     for s in (6, 7):
         piece(base, send_d.at[s], mate).wait_send()
-    for s in range(2 * SUB):
-        part(base, 0, send_d.at[8 + s], 2, mate).wait_send()
+    for i in range(2):
+        for r in range(SUB):
+            part(base, r, send_d.at[8 + i * SUB + r], 2, mate).wait_send()
     for k in range(8):
         lpart(me, 0, hl if k in (3, 4) else nl, k, 0, mate).wait_send()
 
@@ -269,7 +271,7 @@
 
     def write(src, dst):
         copies.append(pltpu.make_async_copy(src, dst, r_sem.at[len(copies)]))
-        copies[-1].start()
+        copies[-1].start(priority=len(copies) % 2)
 
     chips = n // 2
     far = me // 2 + chips // 2

time: 57 us -> 56.8 us (level)
  no operation moved by 1% of the time
where the time goes in v8:
time: 56.8 us; the launch traced here: 56.7 us
  Pallas kernels  56.1 us (99%)
  between operations  0.64 us (1%)
    pallas_call x1, Pallas kernels, local_step(): pl.pallas_call(functools.partial(_gather_kernel, n), out_shape=(pltpu.VME...  44.3 us
    pallas_call x1, Pallas kernels, local_step(): pl.pallas_call(functools.partial(_write_kernel, n), out_shape=(jax.ShapeD...  11.8 us

profile of v8, /device:TPU:113, one launch (start us, length us, event | category | flops | bytes accessed | tf_op | source)
XLA Modules:
  0.0 56.7 jit_solution(7959705755102207755)
XLA Ops:
  0.6 44.3 %shard_map.76 = (f32[1024,8192]{1,0:T(8,128)S(1)}, f32[1088,512]{1,0:T(8,128)S(1)}, bf16[512,512]{1,0:T(8,128)(2,1)S(1)}, bf16[32,512,256]{2,1,0:T(8,128)(2,1)S(...) custom-call(bf16[512,1024]{1,0:T(8,128)(2,1)} %grad.1, bf16[64,512]{1,0:T(8,128)(2,1)} %lroot.1, ...), custom_call_target="tpu_custom_call" | custom-call | tf_op jit(solution)/shard_map/pallas_call | solution.py:315
  44.9 11.8 %shard_map.77 = (f32[1024,8192]{1,0:T(8,128)}, f32[64,512]{1,0:T(8,128)}, f32[512,1024]{1,0:T(8,128)}) custom-call(f32[1024,8192]{1,0:T(8,128)S(1)} %get-tuple-element.12.rbuf, f32[1088,512]{1,0:T(8,128)S(1)} %get-tuple-element.13.xacc, bf16[512,512]{1,0:T(8,128)(2,1)S(1)} %get-tuple-element.14.lbuf, bf16[32,512,256]{2,1,0:T(8,128)(2,1)S(1)} %get-tuple-element.15.gbuf, ...), custom_call_target="tpu_custom_call" | custom-call | tf_op jit(solution)/shard_map/pallas_call | solution.py:329

commit v9 on v8

v9 whole, which is shorter than its diff:
```python
import functools

import jax
import jax.numpy as jnp
from jax import lax
from jax.experimental import pallas as pl
from jax.experimental.pallas import tpu as pltpu
from jax.sharding import PartitionSpec as P

EMA_DECAY = 0.9
SPLIT = 4
SUB = 2
AHEAD = 3
GRANT = 12 << 20

MESH = pl.DeviceIdType.MESH
ANY = pl.BlockSpec(memory_space=pl.ANY)
VMEM = pl.BlockSpec(memory_space=pltpu.VMEM)


def _nt(a, b):
    return lax.dot_general(a, b, (((1,), (1,)), ((), ())), preferred_element_type=jnp.float32)


def _slot(n, me, t, u, i):
    mate = me + 1 - 2 * (me % 2)
    base = jnp.where(u == 0, me, mate)
    s = t - 2
    far = 2 + 2 * (s // SPLIT)
    owner = jnp.where(i == 0, base - far, base + far)
    part = (s + 2 * i) % SPLIT
    owner = jnp.where(t == 0, me, jnp.where(t == 1, mate, owner))
    part = jnp.where(t < 2, 2 * u + i, part)
    return lax.rem(owner + n, n) * SPLIT + part


def _gather_kernel(n, grad, lroot, right, rroot, rbuf, xacc, gbuf, gt, rr,
                   own_sem, l_sem, r_sem, rr_sem, recv, recv_sub, send_p, send_m, send_d):
    me = lax.axis_index("tensor")
    mate = me + 1 - 2 * (me % 2)
    width = gbuf.shape[2]
    cols, rows = gt.shape
    nl = lroot.shape[0]
    body, whole = pl.ds(0, rows), pl.ds(0, rows + nl)
    steps = 6
    ring = lambda d: lax.rem(d + n, n)
    plus, minus = ring(me + 2), ring(me - 2)

    slot = functools.partial(_slot, n, me)

    def span(sl):
        return pl.ds(pl.multiple_of(sl * width, width), width)

    def r_copy(sl):
        return pltpu.make_async_copy(right.at[:, span(sl)], rbuf.at[:, span(sl)], r_sem.at[sl])

    def rr_copy(sl, k):
        return pltpu.make_async_copy(rroot.at[:, span(sl)], rr.at[k, pl.ds(0, cols)], rr_sem.at[k])

    def own_copy(q):
        return pltpu.make_async_copy(grad.at[:, pl.ds(q * width, width)], gbuf.at[me * SPLIT + q, body], own_sem.at[q])

    def left_copy(q):
        half = (q + q // 2) % 2
        return pltpu.make_async_copy(
            lroot.at[:, pl.ds(half * width, width)], gbuf.at[me * SPLIT + q, pl.ds(rows, nl)], l_sem.at[q])

    def send(at, sem, recv_sem, dev):
        return pltpu.make_async_remote_copy(
            src_ref=at, dst_ref=at, send_sem=sem, recv_sem=recv_sem,
            device_id={"tensor": dev}, device_id_type=MESH)

    def piece(sl, sem, dev):
        return send(gbuf.at[sl, whole], sem, recv.at[sl], dev)

    def pair(sl, span_rows, sem, dev):
        return send(gbuf.at[pl.ds(sl, 2), span_rows], sem, recv.at[sl], dev)

    def part(sl, r, sem, group, dev):
        first = rows * 3 // 4
        at = gbuf.at[sl, pl.ds(0, first) if r == 0 else pl.ds(first, rows - first)]
        return send(at, sem, recv_sub.at[group, r], dev)

    own = [[own_copy(q), left_copy(q)] for q in range(SPLIT)]
    for q in (0, 1, 2, 3):
        for c in own[q]:
            c.start()

    def loads(t, k0):
        for u in range(2):
            for i in range(2):
                sl = slot(t, u, i)
                r_copy(sl).start()
                rr_copy(sl, k0 + 2 * u + i).start()

    barrier = pltpu.get_barrier_semaphore()
    for dev in (plus, minus, mate):
        pl.semaphore_signal(barrier, inc=1, device_id={"tensor": dev}, device_id_type=MESH)
    pl.semaphore_wait(barrier, 3)

    base = me * SPLIT
    for q in (0, 1):
        for c in own[q]:
            c.wait()
    pair(base, whole, send_p.at[0], plus).start()
    for q in (2, 3):
        for c in own[q]:
            c.wait()
    pair(base + 2, whole, send_m.at[0], minus).start()
    pair(base + 2, body, send_p.at[1], plus).start()
    pair(base, body, send_m.at[1], minus).start()
    pair(base, whole, send_d.at[0], mate).start()
    pair(base + 2, body, send_d.at[1], mate).start()
    for t in range(AHEAD):
        loads(t, 4 * t)
    for q in range(SPLIT):
        gt[pl.ds(q * width, width), :] = gbuf[me * SPLIT + q, body, :].T
    xacc[...] = jnp.zeros_like(xacc)

    lrow = pl.ds(pl.multiple_of(me * nl, nl), nl)

    def ready(t, u, k0):
        for i in range(2):
            sl = slot(t, u, i)
            r_copy(sl).wait()
            rr_copy(sl, k0 + i).wait()
            rr[k0 + i, pl.ds(cols, nl), :] = gbuf[sl, lrow, :]

    def unit(t, u, k0):
        ready(t, u, k0)
        sls = [slot(t, u, i) for i in range(2)]
        for sl in sls:
            rbuf[:, span(sl)] = EMA_DECAY * rbuf[:, span(sl)] + (1.0 - EMA_DECAY) * jnp.dot(
                gt[...], gbuf[sl, body, :], preferred_element_type=jnp.float32)
        xacc[...] += _nt(rr[k0], gbuf[sls[0], body, :]) + _nt(rr[k0 + 1], gbuf[sls[1], body, :])

    def arrived(sl):
        piece(sl, send_d.at[0], mate).wait_recv()

    def pair_arrived(sl, span_rows):
        pair(sl, span_rows, send_d.at[0], mate).wait_recv()

    def take(t):
        s = t - 2

        @pl.when(t == 1)
        def _():
            pair_arrived(mate * SPLIT, whole)
            pair_arrived(mate * SPLIT + 2, body)

        @pl.when(t >= 2)
        def _():
            a, b = slot(t, 0, 0), slot(t, 0, 1)

            for at, span_rows in ((0, whole), (2, body)):
                @pl.when(s == at)
                def _(span_rows=span_rows):
                    pair_arrived(a, span_rows)
                    pair(a, span_rows, send_d.at[2 + s], mate).start()
                    pair_arrived(b, span_rows)
                    pair(b, span_rows, send_d.at[3 + s], mate).start()

            @pl.when(s == 4)
            def _():
                arrived(a)
                piece(a, send_d.at[6], mate).start()
                arrived(b)
                piece(b, send_d.at[7], mate).start()

            @pl.when(s == 1)
            def _():
                piece(a - 1, send_p.at[2], plus).start()
                piece(b - 1, send_m.at[2], minus).start()
                for r in range(SUB):
                    part(a, r, send_p.at[3 + r], 0, plus).start()
                    part(b, r, send_m.at[3 + r], 1, minus).start()

    def take_last(t):
        for r in range(SUB):
            for i in range(2):
                sl = slot(t, 0, i)
                part(sl, r, send_d.at[0], i, mate).wait_recv()
                part(sl, r, send_d.at[8 + i * SUB + r], 2 + i, mate).start()

    def take_mate(t):
        s = t - 2

        for at, span_rows in ((0, whole), (2, body)):
            @pl.when(s == at)
            def _(span_rows=span_rows):
                pair_arrived(slot(t, 1, 0), span_rows)
                pair_arrived(slot(t, 1, 1), span_rows)

        @pl.when(s == 4)
        def _():
            arrived(slot(t, 1, 0))
            arrived(slot(t, 1, 1))

    def step(t, carry):
        k0 = 4 * lax.rem(t, AHEAD)
        take(t)
        unit(t, 0, k0)
        take_mate(t)
        unit(t, 1, k0 + 2)

        @pl.when(t + AHEAD < steps + 2)
        def _():
            loads(t + AHEAD, k0)
        return carry

    lax.fori_loop(0, steps + 1, step, 0)
    last = steps + 1
    k0 = 4 * (last % AHEAD)
    take_last(last)
    ready(last, 0, k0)
    for r in range(SUB):
        for i in range(2):
            part(slot(last, 1, i), r, send_d.at[0], 2 + i, mate).wait_recv()
    ready(last, 1, k0 + 2)

    for s, span_rows in enumerate((whole, body)):
        pair(base, span_rows, send_p.at[s], plus).wait_send()
        pair(base, span_rows, send_m.at[s], minus).wait_send()
    piece(base, send_p.at[2], plus).wait_send()
    piece(base, send_m.at[2], minus).wait_send()
    for r in range(SUB):
        part(base, r, send_p.at[3 + r], 0, plus).wait_send()
        part(base, r, send_m.at[3 + r], 1, minus).wait_send()
    for s, span_rows in enumerate((whole, body, whole, whole, body, body)):
        pair(base, span_rows, send_d.at[s], mate).wait_send()
    for s in (6, 7):
        piece(base, send_d.at[s], mate).wait_send()
    for i in range(2):
        for r in range(SUB):
            part(base, r, send_d.at[8 + i * SUB + r], 2, mate).wait_send()


def _write_kernel(n, rbuf, xacc, gbuf, gt, rr, left, r_out, l_out, d_out,
                  tail, xs, d_buf, l_buf, lbuf, r_sem, sem):
    me = lax.axis_index("tensor")
    width = gbuf.shape[2]
    cols, nl = d_buf.shape[1], left.shape[0]
    rows = d_buf.shape[0]
    body = pl.ds(0, rows)
    last = 7
    k0 = 4 * (last % AHEAD)

    def span(sl):
        return pl.ds(pl.multiple_of(sl * width, width), width)

    left_copy = pltpu.make_async_copy(left, l_buf, sem.at[0])
    left_copy.start()
    copies = []

    def write(src, dst):
        copies.append(pltpu.make_async_copy(src, dst, r_sem.at[len(copies)]))
        copies[-1].start()

    chips = n // 2
    far = me // 2 + chips // 2
    tall, wide = cols // 4, 2 * cols
    for c in range(1, chips):
        at = pl.ds(pl.multiple_of(lax.rem(far + c, chips) * wide, wide), wide)
        for p in range(4):
            block = (pl.ds(p * tall, tall), at)
            write(rbuf.at[block], r_out.at[block])
    for u in range(2):
        for i in range(2):
            at = span(_slot(n, me, last - 1, u, i))
            write(rbuf.at[:, at], r_out.at[:, at])
    tails = [_slot(n, me, last, u, i) for u in range(2) for i in range(2)]
    for k, sl in enumerate(tails):
        tail[k] = EMA_DECAY * rbuf[:, span(sl)] + (1.0 - EMA_DECAY) * jnp.dot(
            gt[...], gbuf[sl, body, :], preferred_element_type=jnp.float32)
        write(tail.at[k], r_out.at[:, span(sl)])
    g = [gbuf[sl, body, :] for sl in tails]
    xs[...] = xacc[...] + _nt(rr[k0], g[0]) + _nt(rr[k0 + 1], g[1])
    xs[...] += _nt(rr[k0 + 2], g[2]) + _nt(rr[k0 + 3], g[3])
    mate = me + 1 - 2 * (me % 2)
    for near in (me, mate):
        for shift, parts in ((0, (0, 1)), (-2, (0, 1)), (2, (3, 2)), (4, (0, 2))):
            owner = lax.rem(near + shift + n, n)
            at = pl.ds(pl.multiple_of(owner * nl, nl), nl)
            for h, q in enumerate(parts):
                lbuf[at, pl.ds(h * width, width)] = gbuf[owner * SPLIT + q, pl.ds(rows, nl), :]
    d_buf[...] = _nt(lbuf[...], xs[pl.ds(0, cols), :].astype(jnp.bfloat16))
    write(d_buf, d_out)
    left_copy.wait()
    l_buf[...] = EMA_DECAY * l_buf[...] + (1.0 - EMA_DECAY) * xs[pl.ds(cols, nl), :]
    write(l_buf, l_out)
    for c in copies:
        c.wait()


def solution(mesh):
    row_spec = P(("layer", "tensor"), None)
    col_spec = P("layer", "tensor")
    n = mesh.shape["tensor"]

    def local_step(grad, left, right, lroot, rroot):
        rows, cols = grad.shape
        nl = lroot.shape[0]
        width = cols // SPLIT
        f32, bf16 = jnp.float32, jnp.bfloat16
        dma = pltpu.SemaphoreType.DMA
        held = pl.pallas_call(
            functools.partial(_gather_kernel, n),
            out_shape=(pltpu.VMEM(right.shape, f32), pltpu.VMEM((cols + nl, rows), f32),
                       pltpu.VMEM((n * SPLIT, rows + nl, width), bf16), pltpu.VMEM((cols, rows), bf16),
                       pltpu.VMEM((4 * AHEAD, cols + nl, width), bf16)),
            in_specs=[ANY] * 4,
            out_specs=(VMEM,) * 5,
            scratch_shapes=[
                dma((SPLIT,)), dma((SPLIT,)), dma((n * SPLIT,)), dma((4 * AHEAD,)), dma((n * SPLIT,)),
                dma((4, SUB)), dma((3 + SUB,)), dma((3 + SUB,)), dma((8 + 2 * SUB,)),
            ],
            compiler_params=pltpu.CompilerParams(collective_id=0, has_side_effects=True, vmem_limit_bytes=GRANT),
        )(grad, lroot, right, rroot)
        r, l, d = pl.pallas_call(
            functools.partial(_write_kernel, n),
            out_shape=(jax.ShapeDtypeStruct(right.shape, f32), jax.ShapeDtypeStruct((nl, rows), f32),
                       jax.ShapeDtypeStruct((rows, cols), f32)),
            in_specs=[VMEM] * 5 + [ANY],
            out_specs=(ANY,) * 3,
            scratch_shapes=[pltpu.VMEM((4, cols, width), f32), pltpu.VMEM((cols + nl, rows), f32),
                            pltpu.VMEM((rows, cols), f32), pltpu.VMEM((nl, rows), f32), pltpu.VMEM((rows, rows), bf16), dma((22,)), dma((1,))],
            compiler_params=pltpu.CompilerParams(vmem_limit_bytes=GRANT),
        )(*[pltpu.with_memory_space_constraint(v, pltpu.VMEM) for v in held], left)
        return l, r, d

    return jax.shard_map(local_step, mesh=mesh, in_specs=(col_spec, row_spec, row_spec, row_spec, row_spec), out_specs=(row_spec, row_spec, col_spec), check_vma=False)
```

time: 56.8 us -> 56.7 us (level)
  no operation moved by 1% of the time
where the time goes in v9:
time: 56.7 us; the launch traced here: 56.6 us
  Pallas kernels  55.9 us (99%)
  between operations  0.64 us (1%)
    pallas_call x1, Pallas kernels, local_step(): pl.pallas_call(functools.partial(_gather_kernel, n), out_shape=(pltpu.VME...  44.1 us
    pallas_call x1, Pallas kernels, local_step(): pl.pallas_call(functools.partial(_write_kernel, n), out_shape=(jax.ShapeD...  11.8 us

profile of v9, /device:TPU:113, one launch (start us, length us, event | category | flops | bytes accessed | tf_op | source)
XLA Modules:
  0.0 56.6 jit_solution(16131657323827784613)
XLA Ops:
  0.6 44.1 %shard_map.76 = (f32[1024,8192]{1,0:T(8,128)S(1)}, f32[1088,512]{1,0:T(8,128)S(1)}, bf16[32,576,256]{2,1,0:T(8,128)(2,1)S(1)}, bf16[1024,512]{1,0:T(8,128)(2,1)S(1)}, bf16[12,1088,256]{2,1,0:T(8,128)(2,1)S(1)}) custom-call(bf16[512,1024]{1,0:T(8,128)(2,1)} %grad.1, bf16[64,512]{1,0:T(8,128)(2,1)} %lroot.1, f32[1024,8192]{1,0:T(8,128)} %right.1, ...), custom_call_target="tpu_custom_call" | custom-call | tf_op jit(solution)/shard_map/pallas_call | solution.py:306
  44.8 11.8 %shard_map.77 = (f32[1024,8192]{1,0:T(8,128)}, f32[64,512]{1,0:T(8,128)}, f32[512,1024]{1,0:T(8,128)}) custom-call(f32[1024,8192]{1,0:T(8,128)S(1)} %get-tuple-element.11.rbuf, f32[1088,512]{1,0:T(8,128)S(1)} %get-tuple-element.12.xacc, bf16[32,576,256]{2,1,0:T(8,128)(2,1)S(1)} %get-tuple-element.13.gbuf, bf16[1024,512]{1,0:T(8,128)(2,1)S(1)} %get-tuple-element.14.gt, ...), custom_call_target="tpu_custom_call" | custom-call | tf_op jit(solution)/shard_map/pallas_call | solution.py:319

commit v10 on v9

--- a/solution.py
+++ b/solution.py
@@ -9,7 +9,8 @@
 
 EMA_DECAY = 0.9
 SPLIT = 4
-SUB = 2
+CUTS = (0, 384, 464, 512)
+SUB = len(CUTS) - 1
 AHEAD = 3
 GRANT = 12 << 20
 
@@ -45,6 +46,7 @@
     steps = 6
     ring = lambda d: lax.rem(d + n, n)
     plus, minus = ring(me + 2), ring(me - 2)
+    plus_mate, minus_mate = ring(mate + 2), ring(mate - 2)
 
     slot = functools.partial(_slot, n, me)
 
@@ -77,8 +79,7 @@
         return send(gbuf.at[pl.ds(sl, 2), span_rows], sem, recv.at[sl], dev)
 
     def part(sl, r, sem, group, dev):
-        first = rows * 3 // 4
-        at = gbuf.at[sl, pl.ds(0, first) if r == 0 else pl.ds(first, rows - first)]
+        at = gbuf.at[sl, pl.ds(CUTS[r] * rows // CUTS[-1], (CUTS[r + 1] - CUTS[r]) * rows // CUTS[-1])]
         return send(at, sem, recv_sub.at[group, r], dev)
 
     own = [[own_copy(q), left_copy(q)] for q in range(SPLIT)]
@@ -94,9 +95,10 @@
                 rr_copy(sl, k0 + 2 * u + i).start()
 
     barrier = pltpu.get_barrier_semaphore()
-    for dev in (plus, minus, mate):
+    peers = (plus, minus, mate, plus_mate, minus_mate)
+    for dev in peers:
         pl.semaphore_signal(barrier, inc=1, device_id={"tensor": dev}, device_id_type=MESH)
-    pl.semaphore_wait(barrier, 3)
+    pl.semaphore_wait(barrier, len(peers))
 
     base = me * SPLIT
     for q in (0, 1):
@@ -174,13 +176,16 @@
                 for r in range(SUB):
                     part(a, r, send_p.at[3 + r], 0, plus).start()
                     part(b, r, send_m.at[3 + r], 1, minus).start()
+                part(a, SUB - 1, send_p.at[3 + SUB], 2, plus_mate).start()
+                part(b, SUB - 1, send_m.at[3 + SUB], 3, minus_mate).start()
 
     def take_last(t):
         for r in range(SUB):
             for i in range(2):
                 sl = slot(t, 0, i)
                 part(sl, r, send_d.at[0], i, mate).wait_recv()
-                part(sl, r, send_d.at[8 + i * SUB + r], 2 + i, mate).start()
+                if r < SUB - 1:
+                    part(sl, r, send_d.at[8 + i * SUB + r], 2 + i, mate).start()
 
     def take_mate(t):
         s = t - 2
@@ -226,12 +231,14 @@
     for r in range(SUB):
         part(base, r, send_p.at[3 + r], 0, plus).wait_send()
         part(base, r, send_m.at[3 + r], 1, minus).wait_send()
+    part(base, SUB - 1, send_p.at[3 + SUB], 2, plus_mate).wait_send()
+    part(base, SUB - 1, send_m.at[3 + SUB], 3, minus_mate).wait_send()
     for s, span_rows in enumerate((whole, body, whole, whole, body, body)):
         pair(base, span_rows, send_d.at[s], mate).wait_send()
     for s in (6, 7):
         piece(base, send_d.at[s], mate).wait_send()
     for i in range(2):
-        for r in range(SUB):
+        for r in range(SUB - 1):
             part(base, r, send_d.at[8 + i * SUB + r], 2, mate).wait_send()
 
 
@@ -312,7 +319,7 @@
             out_specs=(VMEM,) * 5,
             scratch_shapes=[
                 dma((SPLIT,)), dma((SPLIT,)), dma((n * SPLIT,)), dma((4 * AHEAD,)), dma((n * SPLIT,)),
-                dma((4, SUB)), dma((3 + SUB,)), dma((3 + SUB,)), dma((8 + 2 * SUB,)),
+                dma((4, SUB)), dma((4 + SUB,)), dma((4 + SUB,)), dma((8 + 2 * SUB,)),
             ],
             compiler_params=pltpu.CompilerParams(collective_id=0, has_side_effects=True, vmem_limit_bytes=GRANT),
         )(grad, lroot, right, rroot)

time: 56.7 us -> 56.7 us (level)
  no operation moved by 1% of the time
where the time goes in v10:
time: 56.7 us; the launch traced here: 56.6 us
  Pallas kernels  55.9 us (99%)
  between operations  0.64 us (1%)
    pallas_call x1, Pallas kernels, local_step(): pl.pallas_call(functools.partial(_gather_kernel, n), out_shape=(pltpu.VME...  44.2 us
    pallas_call x1, Pallas kernels, local_step(): pl.pallas_call(functools.partial(_write_kernel, n), out_shape=(jax.ShapeD...  11.8 us

profile of v10, /device:TPU:113, one launch (start us, length us, event | category | flops | bytes accessed | tf_op | source)
XLA Modules:
  0.0 56.6 jit_solution(18347635780126753594)
XLA Ops:
  0.6 44.2 %shard_map.76 = (f32[1024,8192]{1,0:T(8,128)S(1)}, f32[1088,512]{1,0:T(8,128)S(1)}, bf16[32,576,256]{2,1,0:T(8,128)(2,1)S(1)}, bf16[1024,512]{1,0:T(8,128)(2,1)S(1)}, bf16[12,1088,256]{2,1,0:T(8,128)(2,1)S(1)}) custom-call(bf16[512,1024]{1,0:T(8,128)(2,1)} %grad.1, bf16[64,512]{1,0:T(8,128)(2,1)} %lroot.1, f32[1024,8192]{1,0:T(8,128)} %right.1, ...), custom_call_target="tpu_custom_call" | custom-call | tf_op jit(solution)/shard_map/pallas_call | solution.py:313
  44.8 11.8 %shard_map.77 = (f32[1024,8192]{1,0:T(8,128)}, f32[64,512]{1,0:T(8,128)}, f32[512,1024]{1,0:T(8,128)}) custom-call(f32[1024,8192]{1,0:T(8,128)S(1)} %get-tuple-element.11.rbuf, f32[1088,512]{1,0:T(8,128)S(1)} %get-tuple-element.12.xacc, bf16[32,576,256]{2,1,0:T(8,128)(2,1)S(1)} %get-tuple-element.13.gbuf, bf16[1024,512]{1,0:T(8,128)(2,1)S(1)} %get-tuple-element.14.gt, ...), custom_call_target="tpu_custom_call" | custom-call | tf_op jit(solution)/shard_map/pallas_call | solution.py:326

commit v11 on v9

--- a/solution.py
+++ b/solution.py
@@ -45,6 +45,8 @@
     steps = 6
     ring = lambda d: lax.rem(d + n, n)
     plus, minus = ring(me + 2), ring(me - 2)
+    plus_mate, minus_mate = ring(mate + 2), ring(mate - 2)
+    odd = me % 2 == 1
 
     slot = functools.partial(_slot, n, me)
 
@@ -94,9 +96,10 @@
                 rr_copy(sl, k0 + 2 * u + i).start()
 
     barrier = pltpu.get_barrier_semaphore()
-    for dev in (plus, minus, mate):
+    peers = (plus, minus, mate, plus_mate, minus_mate)
+    for dev in peers:
         pl.semaphore_signal(barrier, inc=1, device_id={"tensor": dev}, device_id_type=MESH)
-    pl.semaphore_wait(barrier, 3)
+    pl.semaphore_wait(barrier, len(peers))
 
     base = me * SPLIT
     for q in (0, 1):
@@ -169,11 +172,20 @@
 
             @pl.when(s == 1)
             def _():
+                @pl.when(odd)
+                def _():
+                    part(slot(t, 1, 0), SUB - 1, send_p.at[3 + SUB], 0, plus_mate).start()
+                    part(slot(t, 1, 1), SUB - 1, send_m.at[3 + SUB], 1, minus_mate).start()
                 piece(a - 1, send_p.at[2], plus).start()
                 piece(b - 1, send_m.at[2], minus).start()
-                for r in range(SUB):
+                for r in range(SUB - 1):
                     part(a, r, send_p.at[3 + r], 0, plus).start()
                     part(b, r, send_m.at[3 + r], 1, minus).start()
+
+                @pl.when(odd)
+                def _():
+                    part(a, SUB - 1, send_p.at[2 + SUB], 0, plus).start()
+                    part(b, SUB - 1, send_m.at[2 + SUB], 1, minus).start()
 
     def take_last(t):
         for r in range(SUB):
@@ -223,9 +235,15 @@
         pair(base, span_rows, send_m.at[s], minus).wait_send()
     piece(base, send_p.at[2], plus).wait_send()
     piece(base, send_m.at[2], minus).wait_send()
-    for r in range(SUB):
+    for r in range(SUB - 1):
         part(base, r, send_p.at[3 + r], 0, plus).wait_send()
         part(base, r, send_m.at[3 + r], 1, minus).wait_send()
+
+    @pl.when(odd)
+    def _():
+        for k in (2 + SUB, 3 + SUB):
+            part(base, SUB - 1, send_p.at[k], 0, plus).wait_send()
+            part(base, SUB - 1, send_m.at[k], 1, minus).wait_send()
     for s, span_rows in enumerate((whole, body, whole, whole, body, body)):
         pair(base, span_rows, send_d.at[s], mate).wait_send()
     for s in (6, 7):
@@ -312,7 +330,7 @@
             out_specs=(VMEM,) * 5,
             scratch_shapes=[
                 dma((SPLIT,)), dma((SPLIT,)), dma((n * SPLIT,)), dma((4 * AHEAD,)), dma((n * SPLIT,)),
-                dma((4, SUB)), dma((3 + SUB,)), dma((3 + SUB,)), dma((8 + 2 * SUB,)),
+                dma((4, SUB)), dma((4 + SUB,)), dma((4 + SUB,)), dma((8 + 2 * SUB,)),
             ],
             compiler_params=pltpu.CompilerParams(collective_id=0, has_side_effects=True, vmem_limit_bytes=GRANT),
         )(grad, lroot, right, rroot)

time: 56.7 us -> 56.6 us (level)
  no operation moved by 1% of the time
where the time goes in v11:
time: 56.6 us; the launch traced here: 56.5 us
  Pallas kernels  55.9 us (99%)
  between operations  0.64 us (1%)
    pallas_call x1, Pallas kernels, local_step(): pl.pallas_call(functools.partial(_gather_kernel, n), out_shape=(pltpu.VME...  44.1 us
    pallas_call x1, Pallas kernels, local_step(): pl.pallas_call(functools.partial(_write_kernel, n), out_shape=(jax.ShapeD...  11.8 us

profile of v11, /device:TPU:113, one launch (start us, length us, event | category | flops | bytes accessed | tf_op | source)
XLA Modules:
  0.0 56.5 jit_solution(4786074661525646938)
XLA Ops:
  0.6 44.1 %shard_map.76 = (f32[1024,8192]{1,0:T(8,128)S(1)}, f32[1088,512]{1,0:T(8,128)S(1)}, bf16[32,576,256]{2,1,0:T(8,128)(2,1)S(1)}, bf16[1024,512]{1,0:T(8,128)(2,1)S(1)}, bf16[12,1088,256]{2,1,0:T(8,128)(2,1)S(1)}) custom-call(bf16[512,1024]{1,0:T(8,128)(2,1)} %grad.1, bf16[64,512]{1,0:T(8,128)(2,1)} %lroot.1, f32[1024,8192]{1,0:T(8,128)} %right.1, ...), custom_call_target="tpu_custom_call" | custom-call | tf_op jit(solution)/shard_map/pallas_call | solution.py:324
  44.8 11.8 %shard_map.77 = (f32[1024,8192]{1,0:T(8,128)}, f32[64,512]{1,0:T(8,128)}, f32[512,1024]{1,0:T(8,128)}) custom-call(f32[1024,8192]{1,0:T(8,128)S(1)} %get-tuple-element.11.rbuf, f32[1088,512]{1,0:T(8,128)S(1)} %get-tuple-element.12.xacc, bf16[32,576,256]{2,1,0:T(8,128)(2,1)S(1)} %get-tuple-element.13.gbuf, bf16[1024,512]{1,0:T(8,128)(2,1)S(1)} %get-tuple-element.14.gt, ...), custom_call_target="tpu_custom_call" | custom-call | tf_op jit(solution)/shard_map/pallas_call | solution.py:337

commit v12 on v11

--- a/solution.py
+++ b/solution.py
@@ -79,7 +79,7 @@
         return send(gbuf.at[pl.ds(sl, 2), span_rows], sem, recv.at[sl], dev)
 
     def part(sl, r, sem, group, dev):
-        first = rows * 3 // 4
+        first = rows * 7 // 8
         at = gbuf.at[sl, pl.ds(0, first) if r == 0 else pl.ds(first, rows - first)]
         return send(at, sem, recv_sub.at[group, r], dev)
 

time: 56.6 us -> 57.3 us (1.012)
  Pallas kernels: 55.9 us -> 56.5 us
    pallas_call x1, Pallas kernels: 44.1 us -> 44.7 us  [local_step(): pl.pallas_call(functools.partial(_gather_kernel, n), out_shape=(pltpu.VME...]
where the time goes in v12:
time: 57.3 us; the launch traced here: 57.1 us
  Pallas kernels  56.5 us (99%)
  between operations  0.64 us (1%)
    pallas_call x1, Pallas kernels, local_step(): pl.pallas_call(functools.partial(_gather_kernel, n), out_shape=(pltpu.VME...  44.7 us
    pallas_call x1, Pallas kernels, local_step(): pl.pallas_call(functools.partial(_write_kernel, n), out_shape=(jax.ShapeD...  11.8 us

profile of v12, /device:TPU:113, one launch (start us, length us, event | category | flops | bytes accessed | tf_op | source)
XLA Modules:
  0.0 57.1 jit_solution(12019436792922314507)
XLA Ops:
  0.6 44.7 %shard_map.76 = (f32[1024,8192]{1,0:T(8,128)S(1)}, f32[1088,512]{1,0:T(8,128)S(1)}, bf16[32,576,256]{2,1,0:T(8,128)(2,1)S(1)}, bf16[1024,512]{1,0:T(8,128)(2,1)S(1)}, bf16[12,1088,256]{2,1,0:T(8,128)(2,1)S(1)}) custom-call(bf16[512,1024]{1,0:T(8,128)(2,1)} %grad.1, bf16[64,512]{1,0:T(8,128)(2,1)} %lroot.1, f32[1024,8192]{1,0:T(8,128)} %right.1, ...), custom_call_target="tpu_custom_call" | custom-call | tf_op jit(solution)/shard_map/pallas_call | solution.py:324
  45.4 11.8 %shard_map.77 = (f32[1024,8192]{1,0:T(8,128)}, f32[64,512]{1,0:T(8,128)}, f32[512,1024]{1,0:T(8,128)}) custom-call(f32[1024,8192]{1,0:T(8,128)S(1)} %get-tuple-element.11.rbuf, f32[1088,512]{1,0:T(8,128)S(1)} %get-tuple-element.12.xacc, bf16[32,576,256]{2,1,0:T(8,128)(2,1)S(1)} %get-tuple-element.13.gbuf, bf16[1024,512]{1,0:T(8,128)(2,1)S(1)} %get-tuple-element.14.gt, ...), custom_call_target="tpu_custom_call" | custom-call | tf_op jit(solution)/shard_map/pallas_call | solution.py:337

commit v13 on v12

--- a/solution.py
+++ b/solution.py
@@ -9,7 +9,8 @@
 
 EMA_DECAY = 0.9
 SPLIT = 4
-SUB = 2
+CUTS = (0, 256, 416, 512)
+SUB = len(CUTS) - 1
 AHEAD = 3
 GRANT = 12 << 20
 
@@ -79,8 +80,8 @@
         return send(gbuf.at[pl.ds(sl, 2), span_rows], sem, recv.at[sl], dev)
 
     def part(sl, r, sem, group, dev):
-        first = rows * 7 // 8
-        at = gbuf.at[sl, pl.ds(0, first) if r == 0 else pl.ds(first, rows - first)]
+        first, end = (CUTS[r + k] * rows // CUTS[-1] for k in range(2))
+        at = gbuf.at[sl, pl.ds(first, end - first)]
         return send(at, sem, recv_sub.at[group, r], dev)
 
     own = [[own_copy(q), left_copy(q)] for q in range(SPLIT)]

time: 57.3 us -> 56.7 us (0.990)
  Pallas kernels: 56.5 us -> 55.9 us
where the time goes in v13:
time: 56.7 us; the launch traced here: 56.6 us
  Pallas kernels  55.9 us (99%)
  between operations  0.64 us (1%)
    pallas_call x1, Pallas kernels, local_step(): pl.pallas_call(functools.partial(_gather_kernel, n), out_shape=(pltpu.VME...  44.2 us
    pallas_call x1, Pallas kernels, local_step(): pl.pallas_call(functools.partial(_write_kernel, n), out_shape=(jax.ShapeD...  11.8 us

profile of v13, /device:TPU:113, one launch (start us, length us, event | category | flops | bytes accessed | tf_op | source)
XLA Modules:
  0.0 56.6 jit_solution(8881541332890859666)
XLA Ops:
  0.6 44.2 %shard_map.76 = (f32[1024,8192]{1,0:T(8,128)S(1)}, f32[1088,512]{1,0:T(8,128)S(1)}, bf16[32,576,256]{2,1,0:T(8,128)(2,1)S(1)}, bf16[1024,512]{1,0:T(8,128)(2,1)S(1)}, bf16[12,1088,256]{2,1,0:T(8,128)(2,1)S(1)}) custom-call(bf16[512,1024]{1,0:T(8,128)(2,1)} %grad.1, bf16[64,512]{1,0:T(8,128)(2,1)} %lroot.1, f32[1024,8192]{1,0:T(8,128)} %right.1, ...), custom_call_target="tpu_custom_call" | custom-call | tf_op jit(solution)/shard_map/pallas_call | solution.py:325
  44.8 11.8 %shard_map.77 = (f32[1024,8192]{1,0:T(8,128)}, f32[64,512]{1,0:T(8,128)}, f32[512,1024]{1,0:T(8,128)}) custom-call(f32[1024,8192]{1,0:T(8,128)S(1)} %get-tuple-element.11.rbuf, f32[1088,512]{1,0:T(8,128)S(1)} %get-tuple-element.12.xacc, bf16[32,576,256]{2,1,0:T(8,128)(2,1)S(1)} %get-tuple-element.13.gbuf, bf16[1024,512]{1,0:T(8,128)(2,1)S(1)} %get-tuple-element.14.gt, ...), custom_call_target="tpu_custom_call" | custom-call | tf_op jit(solution)/shard_map/pallas_call | solution.py:338

commit v14 on v13

--- a/solution.py
+++ b/solution.py
@@ -9,7 +9,7 @@
 
 EMA_DECAY = 0.9
 SPLIT = 4
-CUTS = (0, 256, 416, 512)
+CUTS = (0, 352, 464, 512)
 SUB = len(CUTS) - 1
 AHEAD = 3
 GRANT = 12 << 20

time: 56.7 us -> 56.8 us (level)
  no operation moved by 1% of the time
where the time goes in v14:
time: 56.8 us; the launch traced here: 56.7 us
  Pallas kernels  56.1 us (99%)
  between operations  0.64 us (1%)
    pallas_call x1, Pallas kernels, local_step(): pl.pallas_call(functools.partial(_gather_kernel, n), out_shape=(pltpu.VME...  44.3 us
    pallas_call x1, Pallas kernels, local_step(): pl.pallas_call(functools.partial(_write_kernel, n), out_shape=(jax.ShapeD...  11.8 us

profile of v14, /device:TPU:113, one launch (start us, length us, event | category | flops | bytes accessed | tf_op | source)
XLA Modules:
  0.0 56.7 jit_solution(8703370050316224147)
XLA Ops:
  0.6 44.3 %shard_map.76 = (f32[1024,8192]{1,0:T(8,128)S(1)}, f32[1088,512]{1,0:T(8,128)S(1)}, bf16[32,576,256]{2,1,0:T(8,128)(2,1)S(1)}, bf16[1024,512]{1,0:T(8,128)(2,1)S(1)}, bf16[12,1088,256]{2,1,0:T(8,128)(2,1)S(1)}) custom-call(bf16[512,1024]{1,0:T(8,128)(2,1)} %grad.1, bf16[64,512]{1,0:T(8,128)(2,1)} %lroot.1, f32[1024,8192]{1,0:T(8,128)} %right.1, ...), custom_call_target="tpu_custom_call" | custom-call | tf_op jit(solution)/shard_map/pallas_call | solution.py:325
  44.9 11.8 %shard_map.77 = (f32[1024,8192]{1,0:T(8,128)}, f32[64,512]{1,0:T(8,128)}, f32[512,1024]{1,0:T(8,128)}) custom-call(f32[1024,8192]{1,0:T(8,128)S(1)} %get-tuple-element.11.rbuf, f32[1088,512]{1,0:T(8,128)S(1)} %get-tuple-element.12.xacc, bf16[32,576,256]{2,1,0:T(8,128)(2,1)S(1)} %get-tuple-element.13.gbuf, bf16[1024,512]{1,0:T(8,128)(2,1)S(1)} %get-tuple-element.14.gt, ...), custom_call_target="tpu_custom_call" | custom-call | tf_op jit(solution)/shard_map/pallas_call | solution.py:338

commit v15 on v12

--- a/solution.py
+++ b/solution.py
@@ -79,7 +79,7 @@
         return send(gbuf.at[pl.ds(sl, 2), span_rows], sem, recv.at[sl], dev)
 
     def part(sl, r, sem, group, dev):
-        first = rows * 7 // 8
+        first = rows * 5 // 8
         at = gbuf.at[sl, pl.ds(0, first) if r == 0 else pl.ds(first, rows - first)]
         return send(at, sem, recv_sub.at[group, r], dev)
 

time: 57.3 us -> 56.6 us (0.988)
  Pallas kernels: 56.5 us -> 55.8 us
    pallas_call x1, Pallas kernels: 44.7 us -> 44 us  [local_step(): pl.pallas_call(functools.partial(_gather_kernel, n), out_shape=(pltpu.VME...]
where the time goes in v15:
time: 56.6 us; the launch traced here: 56.4 us
  Pallas kernels  55.8 us (99%)
  between operations  0.64 us (1%)
    pallas_call x1, Pallas kernels, local_step(): pl.pallas_call(functools.partial(_gather_kernel, n), out_shape=(pltpu.VME...  44 us
    pallas_call x1, Pallas kernels, local_step(): pl.pallas_call(functools.partial(_write_kernel, n), out_shape=(jax.ShapeD...  11.8 us

profile of v15, /device:TPU:113, one launch (start us, length us, event | category | flops | bytes accessed | tf_op | source)
XLA Modules:
  0.0 56.4 jit_solution(4397438581232121883)
XLA Ops:
  0.6 44.0 %shard_map.76 = (f32[1024,8192]{1,0:T(8,128)S(1)}, f32[1088,512]{1,0:T(8,128)S(1)}, bf16[32,576,256]{2,1,0:T(8,128)(2,1)S(1)}, bf16[1024,512]{1,0:T(8,128)(2,1)S(1)}, bf16[12,1088,256]{2,1,0:T(8,128)(2,1)S(1)}) custom-call(bf16[512,1024]{1,0:T(8,128)(2,1)} %grad.1, bf16[64,512]{1,0:T(8,128)(2,1)} %lroot.1, f32[1024,8192]{1,0:T(8,128)} %right.1, ...), custom_call_target="tpu_custom_call" | custom-call | tf_op jit(solution)/shard_map/pallas_call | solution.py:324
  44.7 11.8 %shard_map.77 = (f32[1024,8192]{1,0:T(8,128)}, f32[64,512]{1,0:T(8,128)}, f32[512,1024]{1,0:T(8,128)}) custom-call(f32[1024,8192]{1,0:T(8,128)S(1)} %get-tuple-element.11.rbuf, f32[1088,512]{1,0:T(8,128)S(1)} %get-tuple-element.12.xacc, bf16[32,576,256]{2,1,0:T(8,128)(2,1)S(1)} %get-tuple-element.13.gbuf, bf16[1024,512]{1,0:T(8,128)(2,1)S(1)} %get-tuple-element.14.gt, ...), custom_call_target="tpu_custom_call" | custom-call | tf_op jit(solution)/shard_map/pallas_call | solution.py:337

commit v16 on v15

--- a/solution.py
+++ b/solution.py
@@ -79,7 +79,7 @@
         return send(gbuf.at[pl.ds(sl, 2), span_rows], sem, recv.at[sl], dev)
 
     def part(sl, r, sem, group, dev):
-        first = rows * 5 // 8
+        first = rows // 2
         at = gbuf.at[sl, pl.ds(0, first) if r == 0 else pl.ds(first, rows - first)]
         return send(at, sem, recv_sub.at[group, r], dev)
 

time: 56.6 us -> 56.8 us (level)
  no operation moved by 1% of the time
where the time goes in v16:
time: 56.8 us; the launch traced here: 56.7 us
  Pallas kernels  56 us (99%)
  between operations  0.64 us (1%)
    pallas_call x1, Pallas kernels, local_step(): pl.pallas_call(functools.partial(_gather_kernel, n), out_shape=(pltpu.VME...  44.3 us
    pallas_call x1, Pallas kernels, local_step(): pl.pallas_call(functools.partial(_write_kernel, n), out_shape=(jax.ShapeD...  11.8 us

profile of v16, /device:TPU:113, one launch (start us, length us, event | category | flops | bytes accessed | tf_op | source)
XLA Modules:
  0.0 56.7 jit_solution(38404316605925037)
XLA Ops:
  0.6 44.3 %shard_map.76 = (f32[1024,8192]{1,0:T(8,128)S(1)}, f32[1088,512]{1,0:T(8,128)S(1)}, bf16[32,576,256]{2,1,0:T(8,128)(2,1)S(1)}, bf16[1024,512]{1,0:T(8,128)(2,1)S(1)}, bf16[12,1088,256]{2,1,0:T(8,128)(2,1)S(1)}) custom-call(bf16[512,1024]{1,0:T(8,128)(2,1)} %grad.1, bf16[64,512]{1,0:T(8,128)(2,1)} %lroot.1, f32[1024,8192]{1,0:T(8,128)} %right.1, ...), custom_call_target="tpu_custom_call" | custom-call | tf_op jit(solution)/shard_map/pallas_call | solution.py:324
  44.9 11.8 %shard_map.77 = (f32[1024,8192]{1,0:T(8,128)}, f32[64,512]{1,0:T(8,128)}, f32[512,1024]{1,0:T(8,128)}) custom-call(f32[1024,8192]{1,0:T(8,128)S(1)} %get-tuple-element.11.rbuf, f32[1088,512]{1,0:T(8,128)S(1)} %get-tuple-element.12.xacc, bf16[32,576,256]{2,1,0:T(8,128)(2,1)S(1)} %get-tuple-element.13.gbuf, bf16[1024,512]{1,0:T(8,128)(2,1)S(1)} %get-tuple-element.14.gt, ...), custom_call_target="tpu_custom_call" | custom-call | tf_op jit(solution)/shard_map/pallas_call | solution.py:337

commit v17 on v16

--- a/solution.py
+++ b/solution.py
@@ -79,7 +79,7 @@
         return send(gbuf.at[pl.ds(sl, 2), span_rows], sem, recv.at[sl], dev)
 
     def part(sl, r, sem, group, dev):
-        first = rows // 2
+        first = rows * 11 // 16
         at = gbuf.at[sl, pl.ds(0, first) if r == 0 else pl.ds(first, rows - first)]
         return send(at, sem, recv_sub.at[group, r], dev)
 

time: 56.8 us -> 56.6 us (level)
  no operation moved by 1% of the time
where the time goes in v17:
time: 56.6 us; the launch traced here: 56.4 us
  Pallas kernels  55.8 us (99%)
  between operations  0.64 us (1%)
    pallas_call x1, Pallas kernels, local_step(): pl.pallas_call(functools.partial(_gather_kernel, n), out_shape=(pltpu.VME...  44 us
    pallas_call x1, Pallas kernels, local_step(): pl.pallas_call(functools.partial(_write_kernel, n), out_shape=(jax.ShapeD...  11.8 us

profile of v17, /device:TPU:113, one launch (start us, length us, event | category | flops | bytes accessed | tf_op | source)
XLA Modules:
  0.0 56.4 jit_solution(16912211324585399628)
XLA Ops:
  0.6 44.0 %shard_map.76 = (f32[1024,8192]{1,0:T(8,128)S(1)}, f32[1088,512]{1,0:T(8,128)S(1)}, bf16[32,576,256]{2,1,0:T(8,128)(2,1)S(1)}, bf16[1024,512]{1,0:T(8,128)(2,1)S(1)}, bf16[12,1088,256]{2,1,0:T(8,128)(2,1)S(1)}) custom-call(bf16[512,1024]{1,0:T(8,128)(2,1)} %grad.1, bf16[64,512]{1,0:T(8,128)(2,1)} %lroot.1, f32[1024,8192]{1,0:T(8,128)} %right.1, ...), custom_call_target="tpu_custom_call" | custom-call | tf_op jit(solution)/shard_map/pallas_call | solution.py:324
  44.7 11.8 %shard_map.77 = (f32[1024,8192]{1,0:T(8,128)}, f32[64,512]{1,0:T(8,128)}, f32[512,1024]{1,0:T(8,128)}) custom-call(f32[1024,8192]{1,0:T(8,128)S(1)} %get-tuple-element.11.rbuf, f32[1088,512]{1,0:T(8,128)S(1)} %get-tuple-element.12.xacc, bf16[32,576,256]{2,1,0:T(8,128)(2,1)S(1)} %get-tuple-element.13.gbuf, bf16[1024,512]{1,0:T(8,128)(2,1)S(1)} %get-tuple-element.14.gt, ...), custom_call_target="tpu_custom_call" | custom-call | tf_op jit(solution)/shard_map/pallas_call | solution.py:337
